TPU v7x, 32 devices: a whole 2x2x4 slice. The times are simulated.
32 devices in a mesh: dp: 8 (over z, y), mp: 4 (over x, core).
Axes of the slice: x: 2, y: 2, z: 4, core: 2. Of those that a mesh axis runs over, the one named last changes fastest.
Arguments:
- tokens: bfloat16 [8, 1024, 1280], P('dp', 'mp'), may hold values from -6 to 6
- sizes: float32 [8, 1024], P('dp'), may hold values from 1 to 8
- ln1_gain: float32 [1280], replicated, may hold values from 0.25 to 1.75
- qkv_weight: bfloat16 [3, 1280, 1280], P(None, 'dp', 'mp'), may hold values from -0.15625 to 0.15625
- proj_weight: bfloat16 [1280, 1280], P('mp', 'dp'), may hold values from -0.15625 to 0.15625
- ln2_gain: float32 [1280], replicated, may hold values from 0.25 to 1.75
- fc1_weight: bfloat16 [1280, 5120], P('dp', 'mp'), may hold values from -0.15625 to 0.15625
- fc1_bias: float32 [5120], P('mp'), may hold values from -3 to 3
- fc2_weight: bfloat16 [5120, 1280], P('mp', 'dp'), may hold values from -0.078125 to 0.078125
- pair_source: int32 [8, 16], P('dp'), may hold values from 0 to 1022, as said below
- pair_target: int32 [8, 16], P('dp'), may hold values from 1 to 1023, as said below
- kept_order: int32 [8, 1008], P('dp'), may hold values from 0 to 1023, as said below
Outputs:
- merged_out: bfloat16 [8, 1008, 1280], P('dp', 'mp')
Inputs may be any that keep to these rules, and one draw needn't show every extreme that they name: `pair_source`: in each image the 16 entries are distinct even token indices. `pair_target`: odd token indices; several sources may join the same target. `kept_order`: in each image every token index that is not in pair_source appears exactly once.
All inputs are finite; a program needn't handle non-finite values.
Results may differ from a plain program's by a relative error of at most 0.017.
Values may be sent and summed in bfloat16 or wider, within the bound.
A program may use at most 64 MiB of HBM per device.

v0:
```python
import functools
import math

import jax
import jax.numpy as jnp
from jax import lax
from jax.experimental import pallas as pl
from jax.experimental.pallas import tpu as pltpu
from jax.sharding import PartitionSpec as P

HEADS = 16


def layer_norm(values, gain):
    center = values - jnp.mean(values, axis=-1, keepdims=True)
    spread = jnp.mean(center * center, axis=-1, keepdims=True)
    return center * lax.rsqrt(spread + 1e-06) * gain


def powers(count):
    bits = []
    bit = 1
    while bit < count:
        bits.append(bit)
        bit *= 2
    return bits


def toggled(index, mask):
    for bit in powers(mask + 1):
        if mask & bit:
            index = index + bit * (1 - 2 * lax.rem(lax.div(index, bit), 2))
    return index


def greet(peers):
    barrier = pltpu.get_barrier_semaphore()
    for axis, peer in peers:
        pl.semaphore_signal(
            barrier, inc=1, device_id={axis: peer}, device_id_type=pl.DeviceIdType.MESH
        )
    pl.semaphore_wait(barrier, len(peers))


class Copies:
    def __init__(self, send, recv):
        self.send, self.recv, self.made = send, recv, []

    def start(self, source, target, axis, peer):
        number = len(self.made)
        copy = pltpu.make_async_remote_copy(
            src_ref=source,
            dst_ref=target,
            send_sem=self.send.at[number],
            recv_sem=self.recv.at[number],
            device_id={axis: peer},
            device_id_type=pl.DeviceIdType.MESH,
        )
        copy.start()
        self.made.append(copy)
        return copy


def rows_of(out, owner, rows):
    span = pl.ds(pl.multiple_of(owner * rows, 16), rows)
    if len(out.shape) == 3:
        return out.at[:, span, :]
    return out.at[span, :]


class Waits:
    def __init__(self):
        self.seen = set()

    def ready(self, copy):
        if id(copy) not in self.seen:
            copy.wait_recv()
            self.seen.add(id(copy))


def dp_peers(dp):
    me = lax.axis_index("dp")
    return me, toggled(me, 1), lax.rem(me + 2, dp), lax.rem(me + dp - 2, dp)


def start_dp(own, out, copies, dp):
    me, pair, after, before = dp_peers(dp)
    here = rows_of(out, me, own.shape[-2])
    return [copies.start(own, here, "dp", peer) for peer in (pair, after, before)]


def relay_dp(own, out, copies, waits, state, dp, step):
    me, pair, after, before = dp_peers(dp)
    ring = dp // 2
    rows = own.shape[-2]
    other, forward, backward = state
    block = rows_of(out, lax.rem(me - 2 * step + 2 * dp, dp), rows)
    waits.ready(forward)
    if step < ring // 2:
        state[1] = copies.start(block, block, "dp", after)
    copies.start(block, block, "dp", pair)
    if step < ring - step:
        block = rows_of(out, toggled(lax.rem(me + 2 * (step - 1), dp), 1), rows)
        waits.ready(other)
        state[0] = copies.start(block, block, "dp", before)
        if step + 1 < ring - step - 1:
            block = rows_of(out, lax.rem(me + 2 * step, dp), rows)
            waits.ready(backward)
            state[2] = copies.start(block, block, "dp", before)


def gather_kernel(dp, mp, *refs):
    own, out = refs[:2], refs[2:4]
    send, recv, local = refs[4:]
    at = lax.axis_index("mp")
    me, pair, after, before = dp_peers(dp)
    greet(
        [("mp", toggled(at, bit)) for bit in powers(mp)]
        + [("dp", pair), ("dp", after), ("dp", before)]
    )
    copies, waits = Copies(send, recv), Waits()
    heads = start_dp(own[1], out[1], copies, dp)
    mine = rows_of(out[0], at, own[0].shape[0])
    bits = list(reversed(powers(mp)))
    here = {bit: copies.start(own[0], mine, "mp", toggled(at, bit)) for bit in bits}
    stays = []
    for number, owner in ((0, at), (1, me)):
        keep = pltpu.make_async_copy(
            own[number], rows_of(out[number], owner, own[number].shape[-2]), local.at[number]
        )
        keep.start()
        stays.append(keep)
    relay_dp(own[1], out[1], copies, waits, heads, dp, 1)
    held = [0]
    for bit in bits:
        for k in list(held):
            if k:
                waits.ready(here[k])
                block = rows_of(out[0], toggled(at, k), own[0].shape[0])
                here[k ^ bit] = copies.start(block, block, "mp", toggled(at, bit))
            held.append(k ^ bit)
    for step in range(2, dp // 4 + 1):
        relay_dp(own[1], out[1], copies, waits, heads, dp, step)
    for copy in copies.made:
        waits.ready(copy)
        copy.wait_send()
    for keep in stays:
        keep.wait()


def gather_all(normed, heads):
    dp, mp = lax.axis_size("dp"), lax.axis_size("mp")
    total = (mp - 1) + (dp - 1)
    shapes = [
        (mp * normed.shape[0], normed.shape[1]),
        (dp * heads.shape[0], heads.shape[1]),
    ]
    return pl.pallas_call(
        functools.partial(gather_kernel, dp, mp),
        out_shape=[jax.ShapeDtypeStruct(shape, jnp.bfloat16) for shape in shapes],
        in_specs=[pl.BlockSpec(memory_space=pltpu.VMEM)] * 2,
        out_specs=[pl.BlockSpec(memory_space=pl.ANY)] * 2,
        scratch_shapes=[
            pltpu.SemaphoreType.DMA((total,)),
            pltpu.SemaphoreType.DMA((total,)),
            pltpu.SemaphoreType.DMA((2,)),
        ],
        compiler_params=pltpu.CompilerParams(collective_id=0, has_side_effects=True),
        cost_estimate=pl.CostEstimate(
            flops=10**10, bytes_accessed=10**8, transcendentals=0
        ),
        name="gather_all",
    )(normed, heads)


def reduce_kernel(dp, mp, last, *refs):
    if last:
        parts, extra, out, held, landing, send, recv = refs
    else:
        parts, extra, own, out, whole, weight, held, landing, normed, send, recv, local = refs
    at = lax.axis_index("mp")
    peers = [("mp", toggled(at, bit)) for bit in powers(mp)]
    if not last:
        peers += [("dp", peer) for peer in dp_peers(dp)[1:]]
    greet(peers)
    copies, waits = Copies(send, recv), Waits()
    slots = 0
    stored = {k: None for k in range(mp)}
    if not last:
        state = start_dp(own, weight, copies, dp)
        rest = pltpu.make_async_copy(
            own, rows_of(weight, lax.axis_index("dp"), own.shape[0]), local.at[1]
        )
        rest.start()

    def source(k):
        return parts.at[toggled(at, k)] if stored[k] is None else held.at[k]

    for bit in powers(mp):
        moving = [k for k in reversed(range(mp)) if k in stored and k & bit]
        flights = []
        for k in moving:
            flights.append(
                (k, slots, copies.start(source(k), landing.at[slots], "mp", toggled(at, bit)))
            )
            slots += 1
        for k, slot, copy in flights:
            waits.ready(copy)
            kept = k ^ bit
            total = source(kept)[...].astype(jnp.float32) + landing[slot].astype(jnp.float32)
            if 2 * bit < mp:
                held[kept] = total.astype(jnp.bfloat16)
                stored[kept] = True
            del stored[k]
        if not last and bit == 1:
            relay_dp(own, weight, copies, waits, state, dp, 1)
    if last:
        out[...] = (extra[...] + total).astype(out.dtype)
    else:
        out[...] = total
        normed[...] = layer_norm(total, extra[...]).astype(jnp.bfloat16)
        keep = pltpu.make_async_copy(normed, whole.at[at], local.at[0])
        keep.start()
        bits = list(reversed(powers(mp)))
        here = {
            bit: copies.start(normed, whole.at[at], "mp", toggled(at, bit)) for bit in bits
        }
        for step in range(2, dp // 4 + 1):
            relay_dp(own, weight, copies, waits, state, dp, step)
        near = [0]
        for bit in bits:
            for k in list(near):
                if k:
                    waits.ready(here[k])
                    block = whole.at[toggled(at, k)]
                    here[k ^ bit] = copies.start(block, block, "mp", toggled(at, bit))
                near.append(k ^ bit)
        keep.wait()
        rest.wait()
    for copy in copies.made:
        waits.ready(copy)
        copy.wait_send()


def reduce_parts(parts, extra, own=None):
    mp, rows, width = parts.shape
    dp = lax.axis_size("dp")
    last = own is None
    operands = [parts, extra] if last else [parts, extra, own]
    vmem = pl.BlockSpec(memory_space=pltpu.VMEM)
    out_shape = [
        jax.ShapeDtypeStruct((rows, width), jnp.bfloat16 if last else jnp.float32)
    ]
    out_specs = [vmem]
    scratch = [
        pltpu.VMEM((mp, rows, width), jnp.bfloat16),
        pltpu.VMEM((mp - 1, rows, width), jnp.bfloat16),
    ]
    total = mp - 1
    if not last:
        out_shape.append(jax.ShapeDtypeStruct((mp, rows, width), jnp.bfloat16))
        out_shape.append(jax.ShapeDtypeStruct((dp * own.shape[0], own.shape[1]), jnp.bfloat16))
        out_specs += [pl.BlockSpec(memory_space=pl.ANY)] * 2
        scratch.append(pltpu.VMEM((rows, width), jnp.bfloat16))
        total = 2 * total + dp - 1
    scratch += [pltpu.SemaphoreType.DMA((total,)), pltpu.SemaphoreType.DMA((total,))]
    if not last:
        scratch.append(pltpu.SemaphoreType.DMA((2,)))
    return pl.pallas_call(
        functools.partial(reduce_kernel, dp, mp, last),
        out_shape=out_shape,
        in_specs=[vmem] * len(operands),
        out_specs=out_specs,
        scratch_shapes=scratch,
        compiler_params=pltpu.CompilerParams(
            collective_id=2 if last else 1, has_side_effects=True
        ),
        cost_estimate=pl.CostEstimate(
            flops=10**10, bytes_accessed=10**8, transcendentals=0
        ),
        name="reduce_last" if last else "reduce_norm_gather",
    )(*operands)


def shards(
    tokens,
    sizes,
    ln1_gain,
    qkv_weight,
    proj_weight,
    ln2_gain,
    fc1_weight,
    fc1_bias,
    fc2_weight,
    pair_source,
    pair_target,
    kept_order,
):
    images, own_tokens, width = tokens.shape
    length = sizes.shape[1]
    kept_total = kept_order.shape[1]
    count = lax.axis_size("mp")
    me = lax.axis_index("mp")
    kept_own = kept_total // count
    padded = -(-kept_own // 16) * 16
    head_size = width // HEADS
    local_width = qkv_weight.shape[2]
    local_heads = local_width // head_size

    base = tokens.astype(jnp.float32)
    normed = layer_norm(base, ln1_gain).astype(jnp.bfloat16)
    whole, heads_whole = gather_all(
        normed.reshape(own_tokens, width),
        jnp.concatenate(
            [qkv_weight[0], qkv_weight[1], qkv_weight[2], proj_weight.T], axis=1
        ),
    )
    whole = whole[None]
    whole, heads_whole, late = lax.optimization_barrier((whole, heads_whole, fc1_weight))
    fc1 = lax.all_gather(late, "dp", axis=0, tiled=True)

    positions = jnp.arange(length, dtype=jnp.int32)
    order = jnp.pad(
        kept_order.reshape(images, count, kept_own),
        ((0, 0), (0, 0), (0, padded - kept_own)),
        constant_values=-1,
    ).reshape(images, count * padded)
    hits = positions[None, None, :] == pair_source[:, :, None]
    destination = positions[None, :] + jnp.sum(
        jnp.where(hits, pair_target[:, :, None] - positions[None, None, :], 0), axis=1
    )
    joins = order[:, :, None] == destination[:, None, :]
    shares = jnp.where(joins, sizes[:, None, :], 0.0)
    merged_size = jnp.sum(shares, axis=2, keepdims=True)
    shares = (shares / jnp.where(merged_size > 0, merged_size, 1.0)).astype(jnp.bfloat16)
    own_shares = lax.dynamic_slice_in_dim(shares, me * own_tokens, own_tokens, 2)

    projected = jnp.einsum(
        "ind,df->inf", whole, heads_whole[:, : 3 * local_width], preferred_element_type=jnp.float32
    ).astype(jnp.bfloat16)
    shaped = [
        projected[:, :, c * local_width : (c + 1) * local_width].reshape(
            images, length, local_heads, head_size
        )
        for c in range(3)
    ]
    size_bias = jnp.log(sizes)[:, None, None, :]
    block = min(512, length)
    outputs = []
    for begin in range(0, length, block):
        scores = (
            jnp.einsum(
                "iqhe,ikhe->ihqk",
                shaped[0][:, begin : begin + block],
                shaped[1],
                preferred_element_type=jnp.float32,
            )
            / math.sqrt(head_size)
            + size_bias
        )
        weights = jax.nn.softmax(scores, axis=-1).astype(jnp.bfloat16)
        outputs.append(
            jnp.einsum("ihqk,ikhe->iqhe", weights, shaped[2], preferred_element_type=jnp.float32)
            .astype(jnp.bfloat16)
            .reshape(images, block, local_width)
        )
    attended = jnp.concatenate(outputs, axis=1)

    joined = jnp.einsum(
        "ijn,ind->ijd", shares, attended, preferred_element_type=jnp.float32
    ).astype(jnp.bfloat16)

    left, right = lax.optimization_barrier(
        (
            jnp.concatenate([joined, own_shares], axis=2),
            jnp.concatenate([heads_whole[:, 3 * local_width :].T, tokens[0]], axis=0),
        )
    )
    parts = jnp.einsum("ijd,de->ije", left, right, preferred_element_type=jnp.float32)
    parts = parts.astype(jnp.bfloat16).reshape(count, padded, width)
    merged, gathered, fc2 = reduce_parts(parts, ln2_gain.reshape(1, width), fc2_weight.T)
    hidden_sum = jnp.einsum(
        "md,df->mf", gathered.reshape(count * padded, width), fc1,
        preferred_element_type=jnp.float32,
    )
    hidden = jax.nn.gelu(hidden_sum + fc1_bias).astype(jnp.bfloat16)
    partial_out = jnp.einsum("mf,df->md", hidden, fc2, preferred_element_type=jnp.float32)
    partial_out = partial_out.astype(jnp.bfloat16).reshape(count, padded, width)
    out = reduce_parts(partial_out, merged)[0]
    return out[None, :kept_own]


def solution(mesh):
    return jax.shard_map(
        shards,
        mesh=mesh,
        in_specs=(
            P("dp", "mp", None),
            P("dp", None),
            P(),
            P(None, "dp", "mp"),
            P("mp", "dp"),
            P(),
            P("dp", "mp"),
            P("mp"),
            P("mp", "dp"),
            P("dp", None),
            P("dp", None),
            P("dp", None),
        ),
        out_specs=P("dp", "mp", None),
        check_vma=False,
    )
```

profile of v0, /device:TPU:0, one launch (start us, length us, event | category | flops | bytes accessed | tf_op | source)
XLA Modules:
  0.0 201.3 jit_solution(8496919089053960590)
XLA Ops:
  6.5 1.1 slice_bitcast_fusion.16
  7.6 1.3 convert_reduce_fusion
  8.9 1.4 fusion.38
  10.3 2.2 %fusion.53.refs_0_ = bf16[256,1280]{1,0:T(8,128)(2,1)} fusion(bf16[1,256,1280]{2,1,0:T(8,128)(2,1)} %param.12, f32[1280]{0:T(1024)} %param.14, f32[256]{0:T(256)S(1)} %add_rsqrt_fusion, f32[256]{0:T(256)S(1)} %broadcast_multiply_fusion), kind=kLoop, calls=%fused_computation.60 | loop fusion | flops 1638400 | bytes 1317888 | tf_op jit(solution)/shard_map/reshape | solution.py:313
  12.5 1.0 concatenate.12.refs_1_
  13.5 45.4 %gather_all.1 = (bf16[1024,1280]{1,0:T(8,128)(2,1)}, bf16[1280,1280]{1,0:T(8,128)(2,1)}) custom-call(bf16[256,1280]{1,0:T(8,128)(2,1)} %fusion.53.refs_0_, bf16[160,1280]{1,0:T(8,128)(2,1)} %concatenate.12.refs_1_), custom_call_target="tpu_custom_call" | custom-call | flops 10000000000 | bytes 100000000 | tf_op jit(solution)/shard_map/gather_all/pallas_call | solution.py:158
  59.2 5.3 %convert_bitcast_fusion = bf16[1,1024,960]{1,2,0:T(8,128)(2,1)S(1)} fusion(bf16[1280,1280]{1,0:T(8,128)(2,1)} %get-tuple-element.18, bf16[1,1024,1280]{2,1,0:T(8,128)(2,1)} %bitcast.112), kind=kOutput, calls=%fused_computation.39 | convolution fusion | flops 2517565440 | bytes 7208960 | tf_op jit(solution)/shard_map/ind,df->inf/dot_general | solution.py:338
  65.2 0.5 broadcast.376
  65.8 0.7 reduce.15
  66.6 2.5 %fusion.51 = (f32[1024]{0:T(1024)S(1)}, f32[1,1024,1024]{1,2,0:T(8,128)}) fusion(f32[1024]{0:T(1024)S(1)} %bitcast.103, s32[1024]{0:T(1024)S(1)} %iota_add_fusion, s32[1024]{0:T(1024)S(1)} %bitcast.105), kind=kLoop, calls=%fused_computation.56 | loop fusion | flops 3144704 | bytes 4210688 | tf_op jit(solution)/shard_map/reduce_sum | solution.py:334
  69.1 4.8 %fusion.68 = (f32[4,512]{1,0:T(4,128)S(1)}, f32[4,512,1024]{2,1,0:T(8,128)}) fusion(f32[1024]{0:T(1024)S(1)} %bitcast.107, bf16[1024,4,80]{0,2,1:T(8,128)(2,1)S(1)} %bitcast.100, bf16[1,1024,4,80]{1,3,2,0:T(8,128)(2,1)S(1)} %bitcast.98), kind=kOutput, calls=%fused_computation.89 | convolution fusion | flops 343933952 | bytes 9383936 | tf_op jit(solution)/shard_map/sub | solution.py:361
  74.0 1.3 fusion.52
  75.3 4.9 %fusion.67 = (f32[4,512]{1,0:T(4,128)S(1)}, f32[4,512,1024]{2,1,0:T(8,128)}) fusion(f32[1024]{0:T(1024)S(1)} %bitcast.108, bf16[1024,4,80]{0,2,1:T(8,128)(2,1)S(1)} %bitcast.101, bf16[1,1024,4,80]{1,3,2,0:T(8,128)(2,1)S(1)} %bitcast.99), kind=kOutput, calls=%fused_computation.88 | convolution fusion | flops 343933952 | bytes 9383936 | tf_op jit(solution)/shard_map/sub | solution.py:361
  80.2 5.0 %fusion.45 = bf16[4,80,512]{2,1,0:T(8,128)(2,1)S(1)} fusion(bf16[1024,4,80]{0,2,1:T(8,128)(2,1)S(1)} %bitcast.96, f32[4,512,1024]{2,1,0:T(8,128)} %get-tuple-element.36, f32[4,512]{1,0:T(4,128)S(1)} %get-tuple-element.35), kind=kOutput, calls=%fused_computation.51 | convolution fusion | flops 339902464 | bytes 9379840 | tf_op jit(solution)/shard_map/ihqk,ikhe->iqhe/dot_general | solution.py:363
  85.2 0.8 copy-done.8
  85.9 1.7 fusion.44
  87.7 1.1 fusion.41
  88.8 1.7 slice_bitcast_fusion
  91.0 0.6 reshape.565.refs_1_
  91.6 3.8 %convolution_convert_fusion = bf16[1024,1280]{1,0:T(8,128)(2,1)} fusion(bf16[576,1280]{0,1:T(8,128)(2,1)S(1)} %pad_maximum_fusion, bf16[1,1024,576]{1,2,0:T(8,128)(2,1)S(1)} %pad_maximum_fusion.1), kind=kOutput, calls=%fused_computation.27 | convolution fusion | flops 1511260160 | bytes 5275648 | tf_op jit(solution)/shard_map/ijd,de->ije/dot_general | solution.py:379
  95.4 61.5 %reduce_norm_gather.1 = (f32[256,1280]{1,0:T(8,128)}, bf16[4,256,1280]{2,1,0:T(8,128)(2,1)}, bf16[1280,1280]{1,0:T(8,128)(2,1)}) custom-call(bf16[4,256,1280]{2,1,0:T(8,128)(2,1)} %bitcast.114, f32[1,1280]{1,0:T(1,128)} %reshape.565.refs_1_, bf16[160,1280]{1,0:T(8,128)(2,1)} %bitcast.111), custom_call_target="tpu_custom_call" | custom-call | flops 10000000000 | bytes 100000000 | tf_op jit(solution)/shard_map/reduce_norm_gather/pallas_call | solution.py:269
  157.0 12.2 %convolution_convert_fusion.1 = bf16[1024,1280]{1,0:T(8,128)(2,1)} fusion(bf16[1280,1280]{1,0:T(8,128)(2,1)} %get-tuple-element.23, bf16[1024,1280]{1,0:T(8,128)(2,1)} %bitcast.113, bf16[1280,1280]{1,0:T(8,128)(2,1)} %all-gather.2.cloned.1.call-done, f32[1280]{0:T(1024)S(1)} %copy-done.7), kind=kOutput, calls=%fused_computation.28 | convolution fusion | flops 6725304320 | bytes 11801600 | tf_op jit(solution)/shard_map/mf,df->md/dot_general | solution.py:387
  169.2 23.3 %reduce_last.1 = bf16[256,1280]{1,0:T(8,128)(2,1)} custom-call(bf16[4,256,1280]{2,1,0:T(8,128)(2,1)} %bitcast.115, f32[256,1280]{1,0:T(8,128)} %get-tuple-element.24.refs_1_), custom_call_target="tpu_custom_call" | custom-call | flops 10000000000 | bytes 100000000 | tf_op jit(solution)/shard_map/reduce_last/pallas_call | solution.py:269
  192.5 2.0 slice_bitcast_fusion.1
  (33 shorter events, 1.8 us)
Async XLA Ops:
  6.5 6.0 %copy-start.1 = (bf16[320,160]{0,1:T(8,128)(2,1)S(1)}, bf16[320,160]{0,1:T(8,128)(2,1)}, u32[]{:S(2)}) copy-start(bf16[320,160]{0,1:T(8,128)(2,1)} %param.16) | copy-start | bytes 307204
  6.5 150.4 %all-gather.2.cloned.1.call-start = ((), (), s32[]{:S(2)}) async-start(), calls=%async_computation | async-start | bytes 3686400 | tf_op jit(solution)/shard_map/all_gather | solution.py:320
  13.5 45.5 %copy-start = (bf16[1,256,1280]{2,1,0:T(8,128)(2,1)S(1)}, bf16[1,256,1280]{2,1,0:T(8,128)(2,1)}, u32[]{:S(2)}) copy-start(bf16[1,256,1280]{2,1,0:T(8,128)(2,1)} %param.12) | copy-start | bytes 1966084
  64.5 0.7 copy-start.2
  64.5 1.2 copy-start.4
  64.6 2.0 copy-start.5
  64.6 2.0 copy-start.6
  80.2 5.8 %copy-start.8 = (f32[4,512,1024]{2,1,0:T(8,128)S(1)}, f32[4,512,1024]{2,1,0:T(8,128)}, u32[]{:S(2)}) copy-start(f32[4,512,1024]{2,1,0:T(8,128)} %get-tuple-element.34) | copy-start | bytes 25165828
  88.7 2.3 %copy-start.3 = (f32[1280]{0:T(1024)S(1)}, f32[1280]{0:T(1024)}, u32[]{:S(2)}) copy-start(f32[1280]{0:T(1024)} %param.17) | copy-start | bytes 15364
  95.4 61.6 %copy-start.7 = (f32[1280]{0:T(1024)S(1)}, f32[1280]{0:T(1024)}, u32[]{:S(2)}) copy-start(f32[1280]{0:T(1024)} %param.19) | copy-start | bytes 15364
Sparse Core Ops, SparseCore 0:
  59.1 75.1 all-gather.1
where the time goes:
time: 202 us; the launch traced here: 201 us
  Pallas kernels  130 us (64%)
  matrix products  38.8 us (19%)
  between operations  13.6 us (7%)
  other arithmetic  10 us (5%)
  local copies, waits for them, and re-layouts  8.58 us (4%)
    pallas_call x2, Pallas kernels, reduce_parts(): pl.pallas_call(functools.partial(reduce_kernel, dp, mp, last), out_shape=...  84.8 us
    pallas_call x1, Pallas kernels, gather_all(): pl.pallas_call(functools.partial(gather_kernel, dp, mp), out_shape=[jax.S...  45.4 us
    dot_general x1, matrix products, shards(): jnp.einsum('mf,df->md', hidden, fc2, preferred_element_type=jnp.float32)  12.2 us
    sub x2, matrix products, shards(): weights = jax.nn.softmax(scores, axis=-1).astype(jnp.bfloat16)  9.7 us
    dot_general x2, matrix products, shards(): jnp.einsum('ihqk,ikhe->iqhe', weights, shaped[2], preferred_element_type=...  6.75 us
    dot_general x1, matrix products, shards(): jnp.einsum('ind,df->inf', whole, heads_whole[:, :3 * local_width], prefer...  5.29 us
  transfers between devices with their start and end apart: 1, of which 0 were waited for; matrix products, arithmetic and copies ran while one was open for 17% of the time, Pallas kernels for 31%

commit v1 on v0

--- a/solution.py
+++ b/solution.py
@@ -390,9 +390,522 @@
     return out[None, :kept_own]
 
 
+LOG2E = math.log2(math.e)
+KINDS = ("E1", "E2", "Y4", "N1", "N2", "M1", "M2", "M3", "M4", "Y1", "Y2", "Y3")
+ARRAYS = ("k", "v", "q", "p", "f1a", "f1b", "f2a", "f2b")
+
+
+def nt_dot(left, right):
+    return lax.dot_general(
+        left, right, (((1,), (1,)), ((), ())), preferred_element_type=jnp.float32
+    )
+
+
+class Streams:
+    def __init__(self, dp, homes, send, recv, local):
+        me = lax.axis_index("dp")
+        z, y = lax.div(me, 2), lax.rem(me, 2)
+        high = lax.div(z, 2)
+        step = 1 - 2 * high
+        self.end = lax.rem(lax.div(z + 1, 2), 2) == 0
+        self.mid = lax.rem(lax.div(z + 1, 2), 2) == 1
+        self.me = me
+        self.pair = z * 2 + 1 - y
+        self.inner = (z + step) * 2 + y
+        self.outer = lax.rem((z - step) * 2 + y + dp, dp)
+        self.ahead = [lax.rem((z + step * k) * 2 + y + dp, dp) for k in range(4)]
+        self.homes, self.send, self.recv, self.local = homes, send, recv, local
+        self.peers = {"inner": self.inner, "outer": self.outer, "pair": self.pair}
+
+    def block(self, name, owner, part=None):
+        source, target, rows = self.homes[name]
+        low, count = 0, rows
+        if part is not None:
+            low, count = part * (rows // 2), rows // 2
+        return target(pl.ds(pl.multiple_of(owner * rows + low, 16), count))
+
+    def own(self, name):
+        return self.homes[name][0]
+
+    def copy(self, name, kind, source, target, peer):
+        number = ARRAYS.index(name) * len(KINDS) + KINDS.index(kind)
+        return pltpu.make_async_remote_copy(
+            src_ref=source,
+            dst_ref=target,
+            send_sem=self.send.at[number],
+            recv_sem=self.recv.at[number],
+            device_id={"dp": self.peers[peer]},
+            device_id_type=pl.DeviceIdType.MESH,
+        )
+
+    def move(self, name, kind, owner, peer, part=None):
+        block = self.block(name, owner, part)
+        self.copy(name, kind, block, block, peer).start()
+
+    def arrived(self, name, *kinds):
+        for kind in kinds:
+            block = self.block(name, self.me, 0 if kind in ("Y4", "M4") else None)
+            self.copy(name, kind, block, block, "pair").wait_recv()
+
+    def stay(self, name):
+        return pltpu.make_async_copy(
+            self.own(name), self.block(name, self.me), self.local.at[ARRAYS.index(name)]
+        )
+
+    def s0(self, name):
+        here = self.block(name, self.me)
+
+        @pl.when(self.end)
+        def _():
+            self.copy(name, "E1", self.own(name), here, "inner").start()
+
+        @pl.when(self.mid)
+        def _():
+            self.copy(name, "M1", self.own(name), here, "outer").start()
+            self.copy(name, "N1", self.own(name), here, "inner").start()
+
+        self.copy(name, "Y1", self.own(name), here, "pair").start()
+        self.stay(name).start()
+
+    def s1(self, name):
+        @pl.when(self.end)
+        def _():
+            self.arrived(name, "M1")
+            self.move(name, "Y4", self.ahead[1], "pair", 0)
+            self.arrived(name, "Y1")
+            self.move(name, "E2", self.pair, "inner")
+
+        @pl.when(self.mid)
+        def _():
+            self.arrived(name, "N1")
+            self.move(name, "M2", self.ahead[1], "outer")
+            self.move(name, "Y2", self.ahead[1], "pair")
+            self.arrived(name, "E1")
+            self.move(name, "N2", self.outer, "inner")
+            self.arrived(name, "Y1")
+            self.move(name, "M4", self.pair, "outer", 1)
+
+    def s2(self, name):
+        @pl.when(self.end)
+        def _():
+            self.arrived(name, "M2")
+            self.move(name, "Y2", self.ahead[2], "pair")
+
+        @pl.when(self.mid)
+        def _():
+            self.arrived(name, "N2")
+            self.move(name, "M3", self.ahead[2], "outer")
+            self.move(name, "Y3", self.ahead[2], "pair")
+
+    def s3(self, name):
+        @pl.when(self.end)
+        def _():
+            self.arrived(name, "M3")
+            self.move(name, "Y3", self.ahead[3], "pair")
+
+    def near(self, name):
+        self.stay(name).wait()
+
+        @pl.when(self.end)
+        def _():
+            self.arrived(name, "M4", "Y4")
+
+        @pl.when(self.mid)
+        def _():
+            self.arrived(name, "E2")
+
+    def far(self, name):
+        self.arrived(name, "Y2", "Y3")
+
+    def full(self, name):
+        self.near(name)
+        self.far(name)
+
+    def sent(self, name):
+        def drain(*kinds):
+            for kind in kinds:
+                block = self.block(name, self.me, 0 if kind in ("Y4", "M4") else None)
+                self.copy(name, kind, block, block, "pair").wait_send()
+
+        drain("Y1", "Y2", "Y3")
+
+        @pl.when(self.end)
+        def _():
+            drain("E1", "E2", "Y4")
+
+        @pl.when(self.mid)
+        def _():
+            drain("N1", "N2", "M1", "M2", "M3", "M4")
+
+
+def column_of(row, count):
+    down = lax.broadcasted_iota(jnp.int32, (count, count), 0)
+    over = lax.broadcasted_iota(jnp.int32, (count, count), 1)
+    return jnp.sum(jnp.where(down == over, row, 0.0), axis=1, keepdims=True)
+
+
+def layer_kernel(dp, mp, kept_own, *refs):
+    (tokens, sizes, gain_one, qkv, proj, gain_two, fc1, bias, fc2, source, target, order) = refs[:12]
+    out = refs[12]
+    (tok, whole, wq, wp, w1, w2, shares, kbuf, qbuf, vbuf, attb, attended, parts, landing,
+     merged, again, hidden, parts_two, landing_two, send, recv, local, msend, mrecv) = refs[13:]
+    rows, width = tok.shape
+    length = sizes.shape[1]
+    local_width = wp.shape[1]
+    local_heads, _, lanes = kbuf.shape
+    head_size = local_width // local_heads
+    half = width // 2
+    at = lax.axis_index("mp")
+    block_of = [toggled(at, k) for k in range(mp)]
+    pair, across = block_of[1], block_of[2]
+
+    cut = fc1.shape[1] // 2
+    shard = fc1.shape[0]
+    homes = {
+        "k": (qkv.at[1], lambda r: wq.at[1, r, :], shard),
+        "v": (qkv.at[2], lambda r: wq.at[2, r, :], shard),
+        "q": (qkv.at[0], lambda r: wq.at[0, r, :], shard),
+        "p": (proj, lambda r: wp.at[r, :], shard),
+        "f1a": (fc1.at[:, pl.ds(0, cut)], lambda r: w1.at[r, pl.ds(0, cut)], shard),
+        "f1b": (fc1.at[:, pl.ds(cut, cut)], lambda r: w1.at[r, pl.ds(cut, cut)], shard),
+        "f2a": (fc2.at[:, pl.ds(0, cut)], lambda r: w2.at[r, pl.ds(0, cut)], shard),
+        "f2b": (fc2.at[:, pl.ds(cut, cut)], lambda r: w2.at[r, pl.ds(cut, cut)], shard),
+    }
+    st = Streams(dp, homes, send, recv, local)
+
+    load = pltpu.make_async_copy(tokens, tok, local.at[len(ARRAYS)])
+    load.start()
+
+    barrier = pltpu.get_barrier_semaphore()
+
+    def hello(axis, peer):
+        pl.semaphore_signal(
+            barrier, inc=1, device_id={axis: peer}, device_id_type=pl.DeviceIdType.MESH
+        )
+
+    hello("mp", pair)
+    hello("mp", across)
+    hello("dp", st.pair)
+    hello("dp", st.inner)
+
+    @pl.when(st.mid)
+    def _():
+        hello("dp", st.outer)
+
+    @pl.when(st.end)
+    def _():
+        pl.semaphore_wait(barrier, 4)
+
+    @pl.when(st.mid)
+    def _():
+        pl.semaphore_wait(barrier, 5)
+
+    st.s0("k")
+    st.s0("v")
+
+    made = []
+
+    def give(src, dst, peer):
+        copy = pltpu.make_async_remote_copy(
+            src_ref=src,
+            dst_ref=dst,
+            send_sem=msend.at[len(made)],
+            recv_sem=mrecv.at[len(made)],
+            device_id={"mp": peer},
+            device_id_type=pl.DeviceIdType.MESH,
+        )
+        copy.start()
+        made.append(copy)
+        return copy
+
+    load.wait()
+    slab = 32
+
+    def norm_rows(i, carry):
+        span = pl.ds(pl.multiple_of(i * slab, slab), slab)
+        whole[at, span, :] = layer_norm(
+            tok[span, :].astype(jnp.float32), gain_one[...]
+        ).astype(jnp.bfloat16)
+        return carry
+
+    lax.fori_loop(0, rows // slab, norm_rows, 0)
+    token_pair = give(whole.at[at], whole.at[at], pair)
+    token_across = give(whole.at[at], whole.at[at], across)
+    st.s0("q")
+
+    position = lax.broadcasted_iota(jnp.int32, (1, length), 1).astype(jnp.float32)
+    count = source.shape[1]
+    source_column = column_of(source[...].astype(jnp.float32), count)
+    target_column = column_of(target[...].astype(jnp.float32), count)
+    destination = position + jnp.sum(
+        jnp.where(position == source_column, target_column - position, 0.0),
+        axis=0,
+        keepdims=True,
+    )
+    size_row = sizes[...]
+    order_row = order[...].astype(jnp.float32)
+
+    def table(b, carry):
+        shape = (rows, order.shape[1])
+        down = lax.broadcasted_iota(jnp.int32, shape, 0)
+        over = lax.broadcasted_iota(jnp.int32, shape, 1)
+        mine = jnp.logical_and(over == down + b * kept_own, down < kept_own)
+        wanted = jnp.sum(jnp.where(mine, order_row + 1.0, 0.0), axis=1, keepdims=True) - 1.0
+        share = jnp.where(wanted == destination, size_row, 0.0)
+        total = jnp.sum(share, axis=1, keepdims=True)
+        share = share / jnp.where(total > 0, total, 1.0)
+        shares[b] = share.astype(jnp.bfloat16)
+        return carry
+
+    lax.fori_loop(0, mp, table, 0)
+    lane = lax.broadcasted_iota(jnp.int32, (length, lanes), 1)
+    for h in range(local_heads):
+        kbuf[h] = jnp.zeros((length, lanes), jnp.bfloat16)
+        qbuf[h] = jnp.zeros((length, lanes), jnp.bfloat16)
+        vbuf[h] = jnp.where(lane == head_size, 1.0, 0.0).astype(jnp.bfloat16)
+    size_bias = jnp.log(size_row) * LOG2E
+
+    st.s1("k")
+    st.s0("p")
+    st.s1("v")
+    st.s2("k")
+    st.s1("q")
+    st.s2("v")
+    st.s3("k")
+    st.s1("p")
+    st.s2("q")
+    st.s3("v")
+    token_across.wait_recv()
+    token_far = give(whole.at[across], whole.at[across], pair)
+    st.s0("f1a")
+    st.s2("p")
+    st.s3("q")
+    st.s0("f1b")
+    token_pair.wait_recv()
+    token_far.wait_recv()
+
+    def project(c, into, factor):
+        def one(b, carry):
+            product = jnp.dot(whole[b], wq[c], preferred_element_type=jnp.float32)
+            if factor != 1.0:
+                product = product * factor
+            product = product.astype(jnp.bfloat16)
+            span = pl.ds(pl.multiple_of(b * rows, rows), rows)
+            for h in range(local_heads):
+                into[h, span, 0:head_size] = product[:, h * head_size : (h + 1) * head_size]
+            return carry
+
+        lax.fori_loop(0, mp, one, 0)
+
+    st.full("k")
+    project(1, kbuf, 1.0)
+    st.s3("p")
+    st.full("v")
+    project(2, vbuf, 1.0)
+    st.full("q")
+    project(0, qbuf, LOG2E / math.sqrt(head_size))
+
+    duties = (
+        (1, st.s1, "f1a"),
+        (3, st.s1, "f1b"),
+        (3, st.s0, "f2a"),
+        (6, st.s2, "f1a"),
+        (8, st.s2, "f1b"),
+        (8, st.s0, "f2b"),
+        (11, st.s3, "f1a"),
+        (13, st.s3, "f1b"),
+        (15, st.s1, "f2a"),
+    )
+
+    def attend(i, carry):
+        for when, duty, name in duties:
+            pl.when(i == when)(functools.partial(duty, name))
+        b, h = lax.div(i, local_heads), lax.rem(i, local_heads)
+        span = pl.ds(pl.multiple_of(b * rows, rows), rows)
+        scores = nt_dot(qbuf[h, span, :], kbuf[h]) + size_bias
+        top = jnp.max(scores, axis=1, keepdims=True)
+        weights = jnp.exp2(scores - top).astype(jnp.bfloat16)
+        mixed = jnp.dot(weights, vbuf[h], preferred_element_type=jnp.float32)
+        attb[h, span, :] = (mixed / mixed[:, head_size : head_size + 1]).astype(jnp.bfloat16)
+        return carry
+
+    lax.fori_loop(0, mp * local_heads, attend, 0)
+    for h in range(local_heads):
+        attended[:, h * head_size : (h + 1) * head_size] = attb[h, :, 0:head_size]
+    st.full("p")
+
+    def part_of(block):
+        share = shares[block]
+        joined = jnp.dot(share, attended[...], preferred_element_type=jnp.float32)
+        kept = shares[block, :, pl.ds(pl.multiple_of(at * rows, rows), rows)]
+        return nt_dot(joined.astype(jnp.bfloat16), wp[...]) + jnp.dot(
+            kept, tok[...], preferred_element_type=jnp.float32
+        )
+
+    parts[2] = part_of(block_of[3]).astype(jnp.bfloat16)
+    first = give(parts.at[2], landing.at[2], pair)
+    mine = part_of(across)
+    first.wait_recv()
+    parts[1] = (mine + landing[2].astype(jnp.float32)).astype(jnp.bfloat16)
+    second = give(parts.at[1], landing.at[1], across)
+    st.s1("f2b")
+    parts[0] = part_of(pair).astype(jnp.bfloat16)
+    third = give(parts.at[0], landing.at[0], pair)
+    merged[...] = part_of(at)
+    st.s2("f2a")
+    third.wait_recv()
+    second.wait_recv()
+    st.s2("f2b")
+
+    def norm_again(i, carry):
+        span = pl.ds(pl.multiple_of(i * slab, slab), slab)
+        total = (
+            merged[span, :]
+            + landing[0, span, :].astype(jnp.float32)
+            + landing[1, span, :].astype(jnp.float32)
+        )
+        merged[span, :] = total
+        again[at, span, :] = layer_norm(total, gain_two[...]).astype(jnp.bfloat16)
+        return carry
+
+    lax.fori_loop(0, rows // slab, norm_again, 0)
+    norm_pair = give(again.at[at], again.at[at], pair)
+    norm_across = give(again.at[at], again.at[at], across)
+    st.s3("f2a")
+    st.s3("f2b")
+    st.full("f1a")
+    st.full("f1b")
+
+    def expand(block):
+        product = jnp.dot(again[block], w1[...], preferred_element_type=jnp.float32)
+        hidden[block] = jax.nn.gelu(product + bias[...]).astype(jnp.bfloat16)
+
+    expand(at)
+    norm_pair.wait_recv()
+    expand(pair)
+    norm_across.wait_recv()
+    norm_far = give(again.at[across], again.at[across], pair)
+    expand(across)
+    norm_far.wait_recv()
+    expand(block_of[3])
+
+    near = lax.div(lax.div(st.me, 2), 2)
+
+    def shrink(number, which):
+        columns = pl.ds(pl.multiple_of(which * half, half), half)
+
+        def piece(block):
+            return nt_dot(hidden[block], w2[columns, :])
+
+        parts_two[number, 2] = piece(block_of[3]).astype(jnp.bfloat16)
+        one = give(parts_two.at[number, 2], landing_two.at[number, 2], pair)
+        mine = piece(across)
+        one.wait_recv()
+        parts_two[number, 1] = (mine + landing_two[number, 2].astype(jnp.float32)).astype(
+            jnp.bfloat16
+        )
+        two = give(parts_two.at[number, 1], landing_two.at[number, 1], across)
+        parts_two[number, 0] = piece(pair).astype(jnp.bfloat16)
+        three = give(parts_two.at[number, 0], landing_two.at[number, 0], pair)
+        merged[:, columns] = merged[:, columns] + piece(at)
+        return columns, two, three
+
+    def finish(number, columns, two, three):
+        three.wait_recv()
+        two.wait_recv()
+        out[:, columns] = (
+            merged[:, columns]
+            + landing_two[number, 0].astype(jnp.float32)
+            + landing_two[number, 1].astype(jnp.float32)
+        ).astype(out.dtype)
+
+    st.near("f2a")
+    st.near("f2b")
+    close = shrink(0, near)
+    st.far("f2a")
+    st.far("f2b")
+    distant = shrink(1, 1 - near)
+    finish(0, *close)
+    finish(1, *distant)
+    for name in ARRAYS:
+        st.sent(name)
+    for copy in made:
+        copy.wait_send()
+
+
+def whole_layer(tokens, sizes, ln1_gain, qkv_weight, proj_weight, ln2_gain, fc1_weight, fc1_bias,
+                fc2_weight, pair_source, pair_target, kept_order):
+    dp, mp = lax.axis_size("dp"), lax.axis_size("mp")
+    _, rows, width = tokens.shape
+    length = sizes.shape[1]
+    kept_own = kept_order.shape[1] // mp
+    local_width = qkv_weight.shape[2]
+    local_heads = HEADS * local_width // width
+    head_size = local_width // local_heads
+    lanes = -(-(head_size + 1) // 128) * 128
+    hidden = fc1_weight.shape[1]
+    bf16, f32 = jnp.bfloat16, jnp.float32
+    vmem = pl.BlockSpec(memory_space=pltpu.VMEM)
+    hbm = pl.BlockSpec(memory_space=pl.ANY)
+    half = width // 2
+    scratch = [
+        pltpu.VMEM((rows, width), bf16),
+        pltpu.VMEM((mp, rows, width), bf16),
+        pltpu.VMEM((3, width, local_width), bf16),
+        pltpu.VMEM((width, local_width), bf16),
+        pltpu.VMEM((width, hidden), bf16),
+        pltpu.VMEM((width, hidden), bf16),
+        pltpu.VMEM((mp, rows, length), bf16),
+        pltpu.VMEM((local_heads, length, lanes), bf16),
+        pltpu.VMEM((local_heads, length, lanes), bf16),
+        pltpu.VMEM((local_heads, length, lanes), bf16),
+        pltpu.VMEM((local_heads, length, lanes), bf16),
+        pltpu.VMEM((length, local_width), bf16),
+        pltpu.VMEM((mp - 1, rows, width), bf16),
+        pltpu.VMEM((mp - 1, rows, width), bf16),
+        pltpu.VMEM((rows, width), f32),
+        pltpu.VMEM((mp, rows, width), bf16),
+        pltpu.VMEM((mp, rows, hidden), bf16),
+        pltpu.VMEM((2, mp - 1, rows, half), bf16),
+        pltpu.VMEM((2, mp - 1, rows, half), bf16),
+        pltpu.SemaphoreType.DMA((len(ARRAYS) * len(KINDS),)),
+        pltpu.SemaphoreType.DMA((len(ARRAYS) * len(KINDS),)),
+        pltpu.SemaphoreType.DMA((len(ARRAYS) + 1,)),
+        pltpu.SemaphoreType.DMA((16,)),
+        pltpu.SemaphoreType.DMA((16,)),
+    ]
+    out = pl.pallas_call(
+        functools.partial(layer_kernel, dp, mp, kept_own),
+        out_shape=jax.ShapeDtypeStruct((rows, width), bf16),
+        in_specs=[hbm, vmem, vmem, hbm, hbm, vmem, hbm, vmem, hbm, vmem, vmem, vmem],
+        out_specs=vmem,
+        scratch_shapes=scratch,
+        compiler_params=pltpu.CompilerParams(
+            collective_id=3, has_side_effects=True, vmem_limit_bytes=60 * 2**20
+        ),
+        cost_estimate=pl.CostEstimate(flops=10**10, bytes_accessed=10**8, transcendentals=0),
+        name="layer",
+    )(
+        tokens.reshape(rows, width),
+        sizes,
+        ln1_gain.reshape(1, width),
+        qkv_weight,
+        proj_weight.T,
+        ln2_gain.reshape(1, width),
+        fc1_weight,
+        fc1_bias.reshape(1, hidden),
+        fc2_weight.T,
+        pair_source,
+        pair_target,
+        kept_order,
+    )
+    return out[None, :kept_own]
+
+
 def solution(mesh):
+    line_by_two = mesh.shape["dp"] == 8 and mesh.shape["mp"] == 4
     return jax.shard_map(
-        shards,
+        whole_layer if line_by_two else shards,
         mesh=mesh,
         in_specs=(
             P("dp", "mp", None),

time: 202 us -> 149 us (0.74)
  matrix products: 38.8 us -> 0 us
  Pallas kernels: 130 us -> 144 us
  between operations: 13.6 us -> 0.01 us
  other arithmetic: 10 us -> 0 us
  local copies, waits for them, and re-layouts: 8.58 us -> 4.58 us
    dot_general x6 -> x0, matrix products: 29.1 us -> none  [the longest x1 12.2 us: shards(): jnp.einsum('mf,df->md', hidden, fc2, preferred_element_type=jnp.float32)]
    pallas_call x3 -> x1, Pallas kernels: 130 us -> 144 us  [whole_layer(): pl.pallas_call(functools.partial(layer_kernel, dp, mp, kept_own), out_sha...]
    sub x2 -> x0, matrix products: 9.7 us -> none  [shards(): weights = jax.nn.softmax(scores, axis=-1).astype(jnp.bfloat16)]
    reduce_sum x4 -> x0, other arithmetic: 5.21 us -> none  [the longest x1 2.47 us: shards(): merged_size = jnp.sum(shares, axis=2, keepdims=True)]
    reshape x1 -> x0, other arithmetic: 2.2 us -> none  [shards(): normed.reshape(own_tokens, width)]
  transfers between devices with their start and end apart: 1 -> 0, of which waited for: 0 -> 0; matrix products, arithmetic and copies ran while one was open for 17% -> 0% of each run, Pallas kernels for 31% -> 0%
where the time goes in v1:
time: 149 us
  Pallas kernels  144 us (97%)
  local copies, waits for them, and re-layouts  4.58 us (3%)
    pallas_call x1, Pallas kernels, whole_layer(): pl.pallas_call(functools.partial(layer_kernel, dp, mp, kept_own), out_sha...  144 us

profile of v1, /device:TPU:0, one launch (start us, length us, event | category | flops | bytes accessed | tf_op | source)
XLA Modules:
  0.0 148.7 jit_solution(15982621141106422744)
XLA Ops:
  0.0 0.0 copy-start
  0.0 1.3 reshape.13.refs_2_
  1.3 0.0 copy-done
  1.3 0.0 copy-start.1
  1.3 0.6 reshape.14.refs_5_
  1.9 0.1 copy-done.1
  2.0 0.6 reshape.15.refs_7_
  2.6 144.1 %layer.1 = bf16[256,1280]{1,0:T(8,128)(2,1)} custom-call(bf16[256,1280]{1,0:T(8,128)(2,1)} %bitcast.5, f32[1,1024]{1,0:T(1,128)} %refs_1_.1, f32[1,1280]{1,0:T(1,128)} %reshape.13.refs_2_, bf16[3,160,320]{2,1,0:T(8,128)(2,1)} %refs_3_.1, bf16[160,320]{1,0:T(8,128)(2,1)} %bitcast.7, f32[1,1280]{1,0:T(1,128)} %reshape.14.refs_5_, bf16[160,1280]{1,0:T(8,128)(2,1)} %refs_6_.1, ...), custom_call_target="tpu_custom_call" | custom-call | flops 10000000000 | bytes 100000000 | tf_op jit(solution)/shard_map/layer/pallas_call | solution.py:877
  146.7 2.0 %slice_bitcast_fusion = bf16[1,252,1280]{2,1,0:T(8,128)(2,1)} fusion(bf16[256,1280]{1,0:T(8,128)(2,1)} %layer.1), kind=kLoop, calls=%fused_computation | loop fusion | bytes 1290240 | tf_op jit(solution)/shard_map/broadcast_in_dim | solution.py:902
Async XLA Ops:
  0.0 1.3 copy-start
  1.3 0.7 copy-start.1

commit v2 on v1

--- a/solution.py
+++ b/solution.py
@@ -392,13 +392,53 @@
 
 LOG2E = math.log2(math.e)
 KINDS = ("E1", "E2", "Y4", "N1", "N2", "M1", "M2", "M3", "M4", "Y1", "Y2", "Y3")
-ARRAYS = ("k", "v", "q", "p", "f1a", "f1b", "f2a", "f2b")
+ARRAYS = ("kv0", "kv1", "pq0", "pq1", "f1a", "f1b", "f2a", "f2b")
+
+SCHEDULE = {
+    "ln": ((("s0", "kv0"), ("s0", "kv1"), ("s0", "pq0")), (("s0", "kv0"), ("s0", "kv1"), ("s0", "pq0"))),
+    "tb": ((("s0", "pq1"), ("M1", "kv0"), ("M1", "pq0"), ("Y1", "pq0"), ("M1", "pq1"), ("M1", "kv1"), ("M2", "kv0"), ("Y1", "kv1"), ("M2", "kv1")), (("s0", "pq1"), ("N1", "kv0"), ("E1", "kv0"), ("E1", "kv1"), ("N1", "kv1"), ("N1", "pq0"), ("E1", "pq1"), ("N1", "pq1"), ("E1", "pq0"), ("N2", "kv0"), ("Y1", "kv1"), ("Y1", "pq1"), ("N2", "kv1"))),
+    "tk": ((("M2", "pq0"),), (("N2", "pq1"),)),
+    "w0": ((("M2", "pq1"), ("Y1", "kv0"), ("M3", "kv0"), ("Y1", "pq1"), ("s0", "f1a"), ("M3", "kv1"), ("M3", "pq1"), ("M3", "pq0")), (("N2", "pq0"), ("Y1", "pq0"), ("Y1", "kv0"), ("s0", "f1a"))),
+    "w1": ((("s0", "f1b"),), ()),
+    "sr": ((("M1", "f1a"),), (("N1", "f1a"),)),
+    "a0": ((("M2", "f1a"),), (("E1", "f1a"),)),
+    "a1": ((), (("s0", "f1b"),)),
+    "a3": ((("Y1", "f1b"),), ()),
+    "a4": ((("s0", "f2a"),), ()),
+    "a6": ((("Y1", "f1a"),), ()),
+    "a7": ((), (("N2", "f1a"),)),
+    "r1": ((("M3", "f1a"),), ()),
+    "a10": ((("M1", "f1b"),), (("N1", "f1b"),)),
+    "a11": ((("M2", "f1b"),), (("E1", "f1b"),)),
+    "a12": ((("Y1", "f2a"),), (("s0", "f2a"),)),
+    "a14": ((), (("Y1", "f1b"),)),
+    "a15": ((), (("Y1", "f1a"),)),
+    "rr": ((("s0", "f2b"), ("M3", "f1b")), (("N2", "f1b"), ("N1", "f2a"), ("E1", "f2a"))),
+    "nm": ((("Y1", "f2b"), ("M2", "f2a")), ()),
+    "e0": ((("M1", "f2b"),), ()),
+    "e1": ((("M1", "f2a"), ("M3", "f2a")), (("s0", "f2b"), ("N2", "f2a"), ("Y1", "f2b"), ("N1", "f2b"), ("Y1", "f2a"), ("E1", "f2b"))),
+    "e2": ((("M2", "f2b"),), ()),
+    "na": ((("M3", "f2b"),), (("N2", "f2b"),)),
+}
 
 
 def nt_dot(left, right):
     return lax.dot_general(
         left, right, (((1,), (1,)), ((), ())), preferred_element_type=jnp.float32
     )
+
+
+START = ((("E1", "inner"), ("Y1", "pair")), (("M1", "outer"), ("N1", "inner"), ("Y1", "pair")))
+RELAY = {
+    (0, "M1"): (("Y4", 1, "pair", 0),),
+    (0, "Y1"): (("E2", "pair", "inner", None),),
+    (0, "M2"): (("Y2", 2, "pair", None),),
+    (0, "M3"): (("Y3", 3, "pair", None),),
+    (1, "N1"): (("M2", 1, "outer", None), ("Y2", 1, "pair", None)),
+    (1, "E1"): (("N2", "outer", "inner", None),),
+    (1, "Y1"): (("M4", "pair", "outer", 1),),
+    (1, "N2"): (("M3", 2, "outer", None), ("Y3", 2, "pair", None)),
+}
 
 
 class Streams:
@@ -413,16 +453,18 @@
         self.pair = z * 2 + 1 - y
         self.inner = (z + step) * 2 + y
         self.outer = lax.rem((z - step) * 2 + y + dp, dp)
+        middle = lax.rem(lax.div(z + 1, 2), 2)
+        self.far = [(z + step * (k - middle)) * 2 for k in (2, 3)]
         self.ahead = [lax.rem((z + step * k) * 2 + y + dp, dp) for k in range(4)]
         self.homes, self.send, self.recv, self.local = homes, send, recv, local
         self.peers = {"inner": self.inner, "outer": self.outer, "pair": self.pair}
 
     def block(self, name, owner, part=None):
-        source, target, rows = self.homes[name]
-        low, count = 0, rows
+        _, target, stride, low, count = self.homes[name]
         if part is not None:
-            low, count = part * (rows // 2), rows // 2
-        return target(pl.ds(pl.multiple_of(owner * rows + low, 16), count))
+            first = -(-count // 32) * 16
+            low, count = low + part * first, (first, count - first)[part]
+        return target(pl.ds(pl.multiple_of(owner * stride + low, 16), count))
 
     def own(self, name):
         return self.homes[name][0]
@@ -444,7 +486,7 @@
 
     def arrived(self, name, *kinds):
         for kind in kinds:
-            block = self.block(name, self.me, 0 if kind in ("Y4", "M4") else None)
+            block = self.block(name, self.me, {"Y4": 0, "M4": 1}.get(kind))
             self.copy(name, kind, block, block, "pair").wait_recv()
 
     def stay(self, name):
@@ -452,59 +494,34 @@
             self.own(name), self.block(name, self.me), self.local.at[ARRAYS.index(name)]
         )
 
-    def s0(self, name):
-        here = self.block(name, self.me)
-
-        @pl.when(self.end)
-        def _():
-            self.copy(name, "E1", self.own(name), here, "inner").start()
-
-        @pl.when(self.mid)
-        def _():
-            self.copy(name, "M1", self.own(name), here, "outer").start()
-            self.copy(name, "N1", self.own(name), here, "inner").start()
-
-        self.copy(name, "Y1", self.own(name), here, "pair").start()
-        self.stay(name).start()
-
-    def s1(self, name):
-        @pl.when(self.end)
-        def _():
-            self.arrived(name, "M1")
-            self.move(name, "Y4", self.ahead[1], "pair", 0)
-            self.arrived(name, "Y1")
-            self.move(name, "E2", self.pair, "inner")
-
-        @pl.when(self.mid)
-        def _():
-            self.arrived(name, "N1")
-            self.move(name, "M2", self.ahead[1], "outer")
-            self.move(name, "Y2", self.ahead[1], "pair")
-            self.arrived(name, "E1")
-            self.move(name, "N2", self.outer, "inner")
-            self.arrived(name, "Y1")
-            self.move(name, "M4", self.pair, "outer", 1)
-
-    def s2(self, name):
-        @pl.when(self.end)
-        def _():
-            self.arrived(name, "M2")
-            self.move(name, "Y2", self.ahead[2], "pair")
-
-        @pl.when(self.mid)
-        def _():
-            self.arrived(name, "N2")
-            self.move(name, "M3", self.ahead[2], "outer")
-            self.move(name, "Y3", self.ahead[2], "pair")
-
-    def s3(self, name):
-        @pl.when(self.end)
-        def _():
-            self.arrived(name, "M3")
-            self.move(name, "Y3", self.ahead[3], "pair")
+    def act(self, role, what, name):
+        if what == "s0":
+            here = self.block(name, self.me)
+            for kind, peer in START[role]:
+                own = here if self.own(name) is None else self.own(name)
+                self.copy(name, kind, own, here, peer).start()
+            if self.own(name) is not None:
+                self.stay(name).start()
+            return
+        self.arrived(name, what)
+        for kind, owner, peer, part in RELAY[role, what]:
+            who = {"pair": self.pair, "outer": self.outer}.get(owner)
+            self.move(name, kind, self.ahead[owner] if who is None else who, peer, part)
+
+    def serve(self, point, when=None):
+        for role, here in ((0, self.end), (1, self.mid)):
+            todo = SCHEDULE.get(point, ((), ()))[role]
+            if todo:
+                condition = here if when is None else jnp.logical_and(when, here)
+
+                @pl.when(condition)
+                def _():
+                    for what, name in todo:
+                        self.act(role, what, name)
 
     def near(self, name):
-        self.stay(name).wait()
+        if self.own(name) is not None:
+            self.stay(name).wait()
 
         @pl.when(self.end)
         def _():
@@ -514,17 +531,14 @@
         def _():
             self.arrived(name, "E2")
 
-    def far(self, name):
-        self.arrived(name, "Y2", "Y3")
-
     def full(self, name):
         self.near(name)
-        self.far(name)
+        self.arrived(name, "Y2", "Y3")
 
     def sent(self, name):
         def drain(*kinds):
             for kind in kinds:
-                block = self.block(name, self.me, 0 if kind in ("Y4", "M4") else None)
+                block = self.block(name, self.me, {"Y4": 0, "M4": 1}.get(kind))
                 self.copy(name, kind, block, block, "pair").wait_send()
 
         drain("Y1", "Y2", "Y3")
@@ -547,11 +561,13 @@
 def layer_kernel(dp, mp, kept_own, *refs):
     (tokens, sizes, gain_one, qkv, proj, gain_two, fc1, bias, fc2, source, target, order) = refs[:12]
     out = refs[12]
-    (tok, whole, wq, wp, w1, w2, shares, kbuf, qbuf, vbuf, attb, attended, parts, landing,
-     merged, again, hidden, parts_two, landing_two, send, recv, local, msend, mrecv) = refs[13:]
+    (tok, raw_qkv, raw_proj, whole, wkv, wpq, w1, w2, shares, picks, own_share, source_share,
+     kbuf, vbuf, qall, qbuf, source_att, attb, joined, parts, landing, merged, again, hidden,
+     near_parts, near_landing, far_parts, far_landing, far_own,
+     send, recv, local, msend, mrecv) = refs[13:]
     rows, width = tok.shape
     length = sizes.shape[1]
-    local_width = wp.shape[1]
+    local_width = joined.shape[1]
     local_heads, _, lanes = kbuf.shape
     head_size = local_width // local_heads
     half = width // 2
@@ -562,19 +578,23 @@
     cut = fc1.shape[1] // 2
     shard = fc1.shape[0]
     homes = {
-        "k": (qkv.at[1], lambda r: wq.at[1, r, :], shard),
-        "v": (qkv.at[2], lambda r: wq.at[2, r, :], shard),
-        "q": (qkv.at[0], lambda r: wq.at[0, r, :], shard),
-        "p": (proj, lambda r: wp.at[r, :], shard),
-        "f1a": (fc1.at[:, pl.ds(0, cut)], lambda r: w1.at[r, pl.ds(0, cut)], shard),
-        "f1b": (fc1.at[:, pl.ds(cut, cut)], lambda r: w1.at[r, pl.ds(cut, cut)], shard),
-        "f2a": (fc2.at[:, pl.ds(0, cut)], lambda r: w2.at[r, pl.ds(0, cut)], shard),
-        "f2b": (fc2.at[:, pl.ds(cut, cut)], lambda r: w2.at[r, pl.ds(cut, cut)], shard),
+        "kv0": (None, lambda r: wkv.at[r, :], shard, 0, shard // 2),
+        "kv1": (None, lambda r: wkv.at[r, :], shard, shard // 2, shard // 2),
+        "pq0": (None, lambda r: wpq.at[r, :], shard, 0, shard // 2),
+        "pq1": (None, lambda r: wpq.at[r, :], shard, shard // 2, shard // 2),
+        "f1a": (fc1.at[:, pl.ds(0, cut)], lambda r: w1.at[r, pl.ds(0, cut)], shard, 0, shard),
+        "f1b": (fc1.at[:, pl.ds(cut, cut)], lambda r: w1.at[r, pl.ds(cut, cut)], shard, 0, shard),
+        "f2a": (fc2.at[:, pl.ds(0, cut)], lambda r: w2.at[r, pl.ds(0, cut)], shard, 0, shard),
+        "f2b": (fc2.at[:, pl.ds(cut, cut)], lambda r: w2.at[r, pl.ds(cut, cut)], shard, 0, shard),
     }
     st = Streams(dp, homes, send, recv, local)
 
     load = pltpu.make_async_copy(tokens, tok, local.at[len(ARRAYS)])
     load.start()
+    load_qkv = pltpu.make_async_copy(qkv, raw_qkv, local.at[len(ARRAYS) + 1])
+    load_qkv.start()
+    load_proj = pltpu.make_async_copy(proj, raw_proj, local.at[len(ARRAYS) + 2])
+    load_proj.start()
 
     barrier = pltpu.get_barrier_semaphore()
 
@@ -583,15 +603,23 @@
             barrier, inc=1, device_id={axis: peer}, device_id_type=pl.DeviceIdType.MESH
         )
 
+    hello("dp", st.pair)
+    hello("dp", st.inner)
     hello("mp", pair)
     hello("mp", across)
-    hello("dp", st.pair)
-    hello("dp", st.inner)
 
     @pl.when(st.mid)
     def _():
         hello("dp", st.outer)
 
+    load_qkv.wait()
+    load_proj.wait()
+    mine = pl.ds(pl.multiple_of(st.me * shard, shard), shard)
+    wkv[mine, 0:local_width] = raw_qkv[1]
+    wkv[mine, local_width : 2 * local_width] = raw_qkv[2]
+    wpq[mine, 0:local_width] = raw_proj[...]
+    wpq[mine, local_width : 2 * local_width] = raw_qkv[0]
+
     @pl.when(st.end)
     def _():
         pl.semaphore_wait(barrier, 4)
@@ -600,8 +628,7 @@
     def _():
         pl.semaphore_wait(barrier, 5)
 
-    st.s0("k")
-    st.s0("v")
+    st.serve("go")
 
     made = []
 
@@ -620,18 +647,21 @@
 
     load.wait()
     slab = 32
+    first_gain = gain_one[...].reshape(1, width)
+    second_gain = gain_two[...].reshape(1, width)
+    first_bias = bias[...].reshape(1, bias.shape[0])
 
     def norm_rows(i, carry):
         span = pl.ds(pl.multiple_of(i * slab, slab), slab)
         whole[at, span, :] = layer_norm(
-            tok[span, :].astype(jnp.float32), gain_one[...]
+            tok[span, :].astype(jnp.float32), first_gain
         ).astype(jnp.bfloat16)
         return carry
 
     lax.fori_loop(0, rows // slab, norm_rows, 0)
     token_pair = give(whole.at[at], whole.at[at], pair)
     token_across = give(whole.at[at], whole.at[at], across)
-    st.s0("q")
+    st.serve("ln")
 
     position = lax.broadcasted_iota(jnp.int32, (1, length), 1).astype(jnp.float32)
     count = source.shape[1]
@@ -645,6 +675,8 @@
     size_row = sizes[...]
     order_row = order[...].astype(jnp.float32)
 
+    picked = (position == source_column).astype(jnp.bfloat16)
+
     def table(b, carry):
         shape = (rows, order.shape[1])
         down = lax.broadcasted_iota(jnp.int32, shape, 0)
@@ -655,107 +687,117 @@
         total = jnp.sum(share, axis=1, keepdims=True)
         share = share / jnp.where(total > 0, total, 1.0)
         shares[b] = share.astype(jnp.bfloat16)
+        here = wanted == position
+        picks[b] = jnp.where(here, 1.0, 0.0).astype(jnp.bfloat16)
+        own_share[b] = jnp.sum(jnp.where(here, share, 0.0), axis=1, keepdims=True)
+        source_share[b] = nt_dot(share.astype(jnp.bfloat16), picked).astype(jnp.bfloat16)
         return carry
 
     lax.fori_loop(0, mp, table, 0)
     lane = lax.broadcasted_iota(jnp.int32, (length, lanes), 1)
     for h in range(local_heads):
         kbuf[h] = jnp.zeros((length, lanes), jnp.bfloat16)
-        qbuf[h] = jnp.zeros((length, lanes), jnp.bfloat16)
+        qbuf[h] = jnp.zeros((rows, lanes), jnp.bfloat16)
         vbuf[h] = jnp.where(lane == head_size, 1.0, 0.0).astype(jnp.bfloat16)
     size_bias = jnp.log(size_row) * LOG2E
 
-    st.s1("k")
-    st.s0("p")
-    st.s1("v")
-    st.s2("k")
-    st.s1("q")
-    st.s2("v")
-    st.s3("k")
-    st.s1("p")
-    st.s2("q")
-    st.s3("v")
+    st.serve("tb")
     token_across.wait_recv()
     token_far = give(whole.at[across], whole.at[across], pair)
-    st.s0("f1a")
-    st.s2("p")
-    st.s3("q")
-    st.s0("f1b")
+    st.serve("tk")
     token_pair.wait_recv()
     token_far.wait_recv()
 
-    def project(c, into, factor):
-        def one(b, carry):
-            product = jnp.dot(whole[b], wq[c], preferred_element_type=jnp.float32)
-            if factor != 1.0:
-                product = product * factor
-            product = product.astype(jnp.bfloat16)
-            span = pl.ds(pl.multiple_of(b * rows, rows), rows)
-            for h in range(local_heads):
-                into[h, span, 0:head_size] = product[:, h * head_size : (h + 1) * head_size]
-            return carry
-
-        lax.fori_loop(0, mp, one, 0)
-
-    st.full("k")
-    project(1, kbuf, 1.0)
-    st.s3("p")
-    st.full("v")
-    project(2, vbuf, 1.0)
-    st.full("q")
-    project(0, qbuf, LOG2E / math.sqrt(head_size))
-
-    duties = (
-        (1, st.s1, "f1a"),
-        (3, st.s1, "f1b"),
-        (3, st.s0, "f2a"),
-        (6, st.s2, "f1a"),
-        (8, st.s2, "f1b"),
-        (8, st.s0, "f2b"),
-        (11, st.s3, "f1a"),
-        (13, st.s3, "f1b"),
-        (15, st.s1, "f2a"),
-    )
-
-    def attend(i, carry):
-        for when, duty, name in duties:
-            pl.when(i == when)(functools.partial(duty, name))
-        b, h = lax.div(i, local_heads), lax.rem(i, local_heads)
+    def project_kv(b, carry):
+        product = jnp.dot(whole[b], wkv[...], preferred_element_type=jnp.float32)
+        product = product.astype(jnp.bfloat16)
         span = pl.ds(pl.multiple_of(b * rows, rows), rows)
-        scores = nt_dot(qbuf[h, span, :], kbuf[h]) + size_bias
+        for h in range(local_heads):
+            low = h * head_size
+            kbuf[h, span, 0:head_size] = product[:, low : low + head_size]
+            low = low + local_width
+            vbuf[h, span, 0:head_size] = product[:, low : low + head_size]
+        return carry
+
+    skip = local_width % 128
+    factor = LOG2E / math.sqrt(head_size)
+
+    def project_q(b, carry):
+        product = jnp.dot(
+            whole[b], wpq[:, local_width - skip :], preferred_element_type=jnp.float32
+        )
+        span = pl.ds(pl.multiple_of(b * rows, rows), rows)
+        qall[span, :] = (product * factor).astype(jnp.bfloat16)
+        return carry
+
+    st.serve("w0")
+    st.full("kv0")
+    st.full("kv1")
+    lax.fori_loop(0, mp, project_kv, 0)
+    st.serve("w1")
+    st.full("pq0")
+    st.full("pq1")
+    lax.fori_loop(0, mp, project_q, 0)
+
+    def heads_of(product):
+        chosen = product.astype(jnp.bfloat16)
+        for h in range(local_heads):
+            low = skip + h * head_size
+            yield h, chosen[:, low : low + head_size]
+
+    def mix(query, h):
+        scores = nt_dot(query, kbuf[h]) + size_bias
         top = jnp.max(scores, axis=1, keepdims=True)
         weights = jnp.exp2(scores - top).astype(jnp.bfloat16)
         mixed = jnp.dot(weights, vbuf[h], preferred_element_type=jnp.float32)
-        attb[h, span, :] = (mixed / mixed[:, head_size : head_size + 1]).astype(jnp.bfloat16)
+        return mixed / mixed[:, head_size : head_size + 1]
+
+    st.serve("sr")
+    product = jnp.dot(picked, qall[...], preferred_element_type=jnp.float32)
+    for h, query in heads_of(product):
+        qbuf[h, 0:count, 0:head_size] = query
+
+    def attend_source(h, carry):
+        source_att[h] = mix(qbuf[h, 0:count, :], h).astype(jnp.bfloat16)
         return carry
 
-    lax.fori_loop(0, mp * local_heads, attend, 0)
-    for h in range(local_heads):
-        attended[:, h * head_size : (h + 1) * head_size] = attb[h, :, 0:head_size]
-    st.full("p")
-
-    def part_of(block):
-        share = shares[block]
-        joined = jnp.dot(share, attended[...], preferred_element_type=jnp.float32)
+    lax.fori_loop(0, local_heads, attend_source, 0)
+
+    def part_of(turn, block):
+        product = jnp.dot(picks[block], qall[...], preferred_element_type=jnp.float32)
+        for h, query in heads_of(product):
+            qbuf[h, :, 0:head_size] = query
+
+        def attend(h, carry):
+            for n in range(local_heads):
+                st.serve(f"a{turn * local_heads + n}", h == n)
+            taken = jnp.dot(
+                source_share[block], source_att[h], preferred_element_type=jnp.float32
+            )
+            attb[h] = (mix(qbuf[h], h) * own_share[block] + taken).astype(jnp.bfloat16)
+            return carry
+
+        lax.fori_loop(0, local_heads, attend, 0)
+        for h in range(local_heads):
+            joined[:, h * head_size : (h + 1) * head_size] = attb[h, :, 0:head_size]
+        st.serve(f"r{turn}")
         kept = shares[block, :, pl.ds(pl.multiple_of(at * rows, rows), rows)]
-        return nt_dot(joined.astype(jnp.bfloat16), wp[...]) + jnp.dot(
+        return nt_dot(joined[...], wpq[:, 0:local_width]) + jnp.dot(
             kept, tok[...], preferred_element_type=jnp.float32
         )
 
-    parts[2] = part_of(block_of[3]).astype(jnp.bfloat16)
+    parts[2] = part_of(0, block_of[3]).astype(jnp.bfloat16)
     first = give(parts.at[2], landing.at[2], pair)
-    mine = part_of(across)
+    total = part_of(1, across)
     first.wait_recv()
-    parts[1] = (mine + landing[2].astype(jnp.float32)).astype(jnp.bfloat16)
+    parts[1] = (total + landing[2].astype(jnp.float32)).astype(jnp.bfloat16)
     second = give(parts.at[1], landing.at[1], across)
-    st.s1("f2b")
-    parts[0] = part_of(pair).astype(jnp.bfloat16)
+    parts[0] = part_of(2, pair).astype(jnp.bfloat16)
     third = give(parts.at[0], landing.at[0], pair)
-    merged[...] = part_of(at)
-    st.s2("f2a")
+    merged[...] = part_of(3, at)
+    st.serve("rr")
     third.wait_recv()
     second.wait_recv()
-    st.s2("f2b")
 
     def norm_again(i, carry):
         span = pl.ds(pl.multiple_of(i * slab, slab), slab)
@@ -765,68 +807,82 @@
             + landing[1, span, :].astype(jnp.float32)
         )
         merged[span, :] = total
-        again[at, span, :] = layer_norm(total, gain_two[...]).astype(jnp.bfloat16)
+        again[at, span, :] = layer_norm(total, second_gain).astype(jnp.bfloat16)
         return carry
 
     lax.fori_loop(0, rows // slab, norm_again, 0)
     norm_pair = give(again.at[at], again.at[at], pair)
     norm_across = give(again.at[at], again.at[at], across)
-    st.s3("f2a")
-    st.s3("f2b")
+    st.serve("nm")
     st.full("f1a")
     st.full("f1b")
 
     def expand(block):
         product = jnp.dot(again[block], w1[...], preferred_element_type=jnp.float32)
-        hidden[block] = jax.nn.gelu(product + bias[...]).astype(jnp.bfloat16)
+        hidden[block] = jax.nn.gelu(product + first_bias).astype(jnp.bfloat16)
 
     expand(at)
+    st.serve("e0")
     norm_pair.wait_recv()
     expand(pair)
+    st.serve("e1")
     norm_across.wait_recv()
     norm_far = give(again.at[across], again.at[across], pair)
+    st.serve("ag")
     expand(across)
+    st.serve("e2")
     norm_far.wait_recv()
     expand(block_of[3])
+    st.serve("e3")
 
     near = lax.div(lax.div(st.me, 2), 2)
 
-    def shrink(number, which):
-        columns = pl.ds(pl.multiple_of(which * half, half), half)
+    def shrink(start, size, ready, landed):
+        columns = pl.ds(pl.multiple_of(start, shard), size)
 
         def piece(block):
             return nt_dot(hidden[block], w2[columns, :])
 
-        parts_two[number, 2] = piece(block_of[3]).astype(jnp.bfloat16)
-        one = give(parts_two.at[number, 2], landing_two.at[number, 2], pair)
-        mine = piece(across)
+        ready[2] = piece(block_of[3]).astype(jnp.bfloat16)
+        one = give(ready.at[2], landed.at[2], pair)
+        total = piece(across)
         one.wait_recv()
-        parts_two[number, 1] = (mine + landing_two[number, 2].astype(jnp.float32)).astype(
-            jnp.bfloat16
-        )
-        two = give(parts_two.at[number, 1], landing_two.at[number, 1], across)
-        parts_two[number, 0] = piece(pair).astype(jnp.bfloat16)
-        three = give(parts_two.at[number, 0], landing_two.at[number, 0], pair)
-        merged[:, columns] = merged[:, columns] + piece(at)
-        return columns, two, three
-
-    def finish(number, columns, two, three):
-        three.wait_recv()
-        two.wait_recv()
-        out[:, columns] = (
-            merged[:, columns]
-            + landing_two[number, 0].astype(jnp.float32)
-            + landing_two[number, 1].astype(jnp.float32)
-        ).astype(out.dtype)
+        ready[1] = (total + landed[2].astype(jnp.float32)).astype(jnp.bfloat16)
+        two = give(ready.at[1], landed.at[1], across)
+        ready[0] = piece(pair).astype(jnp.bfloat16)
+        three = give(ready.at[0], landed.at[0], pair)
+        return piece(at), two, three
+
+    def landed_sum(landed):
+        return landed[0].astype(jnp.float32) + landed[1].astype(jnp.float32)
 
     st.near("f2a")
     st.near("f2b")
-    close = shrink(0, near)
-    st.far("f2a")
-    st.far("f2b")
-    distant = shrink(1, 1 - near)
-    finish(0, *close)
-    finish(1, *distant)
+    span = pl.ds(pl.multiple_of(near * half, half), half)
+    total, *close = shrink(near * half, half, near_parts, near_landing)
+    merged[:, span] = merged[:, span] + total
+    st.serve("na")
+    flights = []
+    for number, kind in ((0, "Y2"), (1, "Y3")):
+        st.arrived("f2a", kind)
+        st.arrived("f2b", kind)
+        total, *flight = shrink(
+            lax.div(st.far[number], 2) * 2 * shard, 2 * shard, far_parts.at[number],
+            far_landing.at[number],
+        )
+        far_own[number] = total
+        flights += flight
+        st.serve(("nc", "nd")[number])
+    for flight in close:
+        flight.wait_recv()
+    out[:, span] = (merged[:, span] + landed_sum(near_landing)).astype(out.dtype)
+    for flight in flights:
+        flight.wait_recv()
+    span = pl.ds(pl.multiple_of((1 - near) * half, half), half)
+    sides = [
+        far_own[side] + landed_sum(far_landing.at[side]) for side in (near, 1 - near)
+    ]
+    out[:, span] = (merged[:, span] + jnp.concatenate(sides, axis=1)).astype(out.dtype)
     for name in ARRAYS:
         st.sent(name)
     for copy in made:
@@ -848,31 +904,43 @@
     vmem = pl.BlockSpec(memory_space=pltpu.VMEM)
     hbm = pl.BlockSpec(memory_space=pl.ANY)
     half = width // 2
+    shard, count = fc1_weight.shape[0], pair_source.shape[1]
+    whole_q = local_width + local_width % 128
     scratch = [
         pltpu.VMEM((rows, width), bf16),
+        pltpu.VMEM((3, shard, local_width), bf16),
+        pltpu.VMEM((shard, local_width), bf16),
         pltpu.VMEM((mp, rows, width), bf16),
-        pltpu.VMEM((3, width, local_width), bf16),
-        pltpu.VMEM((width, local_width), bf16),
+        pltpu.VMEM((width, 2 * local_width), bf16),
+        pltpu.VMEM((width, 2 * local_width), bf16),
         pltpu.VMEM((width, hidden), bf16),
         pltpu.VMEM((width, hidden), bf16),
         pltpu.VMEM((mp, rows, length), bf16),
+        pltpu.VMEM((mp, rows, length), bf16),
+        pltpu.VMEM((mp, rows, 1), f32),
+        pltpu.VMEM((mp, rows, count), bf16),
         pltpu.VMEM((local_heads, length, lanes), bf16),
         pltpu.VMEM((local_heads, length, lanes), bf16),
-        pltpu.VMEM((local_heads, length, lanes), bf16),
-        pltpu.VMEM((local_heads, length, lanes), bf16),
-        pltpu.VMEM((length, local_width), bf16),
+        pltpu.VMEM((length, whole_q), bf16),
+        pltpu.VMEM((local_heads, rows, lanes), bf16),
+        pltpu.VMEM((local_heads, count, lanes), bf16),
+        pltpu.VMEM((local_heads, rows, lanes), bf16),
+        pltpu.VMEM((rows, local_width), bf16),
         pltpu.VMEM((mp - 1, rows, width), bf16),
         pltpu.VMEM((mp - 1, rows, width), bf16),
         pltpu.VMEM((rows, width), f32),
         pltpu.VMEM((mp, rows, width), bf16),
         pltpu.VMEM((mp, rows, hidden), bf16),
-        pltpu.VMEM((2, mp - 1, rows, half), bf16),
-        pltpu.VMEM((2, mp - 1, rows, half), bf16),
+        pltpu.VMEM((mp - 1, rows, half), bf16),
+        pltpu.VMEM((mp - 1, rows, half), bf16),
+        pltpu.VMEM((2, mp - 1, rows, 2 * shard), bf16),
+        pltpu.VMEM((2, mp - 1, rows, 2 * shard), bf16),
+        pltpu.VMEM((2, rows, 2 * shard), f32),
         pltpu.SemaphoreType.DMA((len(ARRAYS) * len(KINDS),)),
         pltpu.SemaphoreType.DMA((len(ARRAYS) * len(KINDS),)),
-        pltpu.SemaphoreType.DMA((len(ARRAYS) + 1,)),
-        pltpu.SemaphoreType.DMA((16,)),
-        pltpu.SemaphoreType.DMA((16,)),
+        pltpu.SemaphoreType.DMA((len(ARRAYS) + 3,)),
+        pltpu.SemaphoreType.DMA((18,)),
+        pltpu.SemaphoreType.DMA((18,)),
     ]
     out = pl.pallas_call(
         functools.partial(layer_kernel, dp, mp, kept_own),
@@ -888,12 +956,12 @@
     )(
         tokens.reshape(rows, width),
         sizes,
-        ln1_gain.reshape(1, width),
+        ln1_gain,
         qkv_weight,
         proj_weight.T,
-        ln2_gain.reshape(1, width),
+        ln2_gain,
         fc1_weight,
-        fc1_bias.reshape(1, hidden),
+        fc1_bias,
         fc2_weight.T,
         pair_source,
         pair_target,

time: 149 us -> 121 us (0.81)
  Pallas kernels: 144 us -> 119 us
  local copies, waits for them, and re-layouts: 4.58 us -> 1.97 us
    pallas_call x1, Pallas kernels: 144 us -> 119 us  [whole_layer(): pl.pallas_call(functools.partial(layer_kernel, dp, mp, kept_own), out_sha...]
    reshape x3 -> x0, local copies, waits for them, and re-layouts: 2.49 us -> none  [the longest x1 1.31 us: whole_layer(): ln1_gain.reshape(1, width)]
where the time goes in v2:
time: 121 us
  Pallas kernels  119 us (98%)
  local copies, waits for them, and re-layouts  1.97 us (2%)
    pallas_call x1, Pallas kernels, whole_layer(): pl.pallas_call(functools.partial(layer_kernel, dp, mp, kept_own), out_sha...  119 us

profile of v2, /device:TPU:0, one launch (start us, length us, event | category | flops | bytes accessed | tf_op | source)
XLA Modules:
  0.0 121.2 jit_solution(12009430345898903347)
XLA Ops:
  0.0 119.2 %layer.1 = bf16[256,1280]{1,0:T(8,128)(2,1)} custom-call(bf16[256,1280]{1,0:T(8,128)(2,1)} %bitcast.5, f32[1,1024]{1,0:T(1,128)} %refs_1_.1, f32[1280]{0:T(1024)} %refs_2_.1, bf16[3,160,320]{2,1,0:T(8,128)(2,1)} %refs_3_.1, bf16[160,320]{1,0:T(8,128)(2,1)} %bitcast.7, f32[1280]{0:T(1024)} %refs_5_.1, bf16[160,1280]{1,0:T(8,128)(2,1)} %refs_6_.1, ...), custom_call_target="tpu_custom_call" | custom-call | flops 10000000000 | bytes 100000000 | tf_op jit(solution)/shard_map/layer/pallas_call | solution.py:945
  119.2 2.0 %slice_bitcast_fusion = bf16[1,252,1280]{2,1,0:T(8,128)(2,1)} fusion(bf16[256,1280]{1,0:T(8,128)(2,1)} %layer.1), kind=kLoop, calls=%fused_computation | loop fusion | bytes 1290240 | tf_op jit(solution)/shard_map/broadcast_in_dim | solution.py:970

commit v3 on v2

--- a/solution.py
+++ b/solution.py
@@ -392,33 +392,35 @@
 
 LOG2E = math.log2(math.e)
 KINDS = ("E1", "E2", "Y4", "N1", "N2", "M1", "M2", "M3", "M4", "Y1", "Y2", "Y3")
-ARRAYS = ("kv0", "kv1", "pq0", "pq1", "f1a", "f1b", "f2a", "f2b")
+E1, E2, Y4, N1, N2, M1, M2, M3, M4, Y1, Y2, Y3 = KINDS
+S0 = "s0"
+ARRAYS = ("kv0", "kv1", "q", "p", "f1a", "f1b", "f2a", "f2b", "f2c")
+W_KV0, W_KV1, W_Q, W_P, W_F1A, W_F1B, W_F2A, W_F2B, W_F2C = ARRAYS
+DOWN = (W_F2A, W_F2B, W_F2C)
 
 SCHEDULE = {
-    "ln": ((("s0", "kv0"), ("s0", "kv1"), ("s0", "pq0")), (("s0", "kv0"), ("s0", "kv1"), ("s0", "pq0"))),
-    "tb": ((("s0", "pq1"), ("M1", "kv0"), ("M1", "pq0"), ("Y1", "pq0"), ("M1", "pq1"), ("M1", "kv1"), ("M2", "kv0"), ("Y1", "kv1"), ("M2", "kv1")), (("s0", "pq1"), ("N1", "kv0"), ("E1", "kv0"), ("E1", "kv1"), ("N1", "kv1"), ("N1", "pq0"), ("E1", "pq1"), ("N1", "pq1"), ("E1", "pq0"), ("N2", "kv0"), ("Y1", "kv1"), ("Y1", "pq1"), ("N2", "kv1"))),
-    "tk": ((("M2", "pq0"),), (("N2", "pq1"),)),
-    "w0": ((("M2", "pq1"), ("Y1", "kv0"), ("M3", "kv0"), ("Y1", "pq1"), ("s0", "f1a"), ("M3", "kv1"), ("M3", "pq1"), ("M3", "pq0")), (("N2", "pq0"), ("Y1", "pq0"), ("Y1", "kv0"), ("s0", "f1a"))),
-    "w1": ((("s0", "f1b"),), ()),
-    "sr": ((("M1", "f1a"),), (("N1", "f1a"),)),
-    "a0": ((("M2", "f1a"),), (("E1", "f1a"),)),
-    "a1": ((), (("s0", "f1b"),)),
-    "a3": ((("Y1", "f1b"),), ()),
-    "a4": ((("s0", "f2a"),), ()),
-    "a6": ((("Y1", "f1a"),), ()),
-    "a7": ((), (("N2", "f1a"),)),
-    "r1": ((("M3", "f1a"),), ()),
-    "a10": ((("M1", "f1b"),), (("N1", "f1b"),)),
-    "a11": ((("M2", "f1b"),), (("E1", "f1b"),)),
-    "a12": ((("Y1", "f2a"),), (("s0", "f2a"),)),
-    "a14": ((), (("Y1", "f1b"),)),
-    "a15": ((), (("Y1", "f1a"),)),
-    "rr": ((("s0", "f2b"), ("M3", "f1b")), (("N2", "f1b"), ("N1", "f2a"), ("E1", "f2a"))),
-    "nm": ((("Y1", "f2b"), ("M2", "f2a")), ()),
-    "e0": ((("M1", "f2b"),), ()),
-    "e1": ((("M1", "f2a"), ("M3", "f2a")), (("s0", "f2b"), ("N2", "f2a"), ("Y1", "f2b"), ("N1", "f2b"), ("Y1", "f2a"), ("E1", "f2b"))),
-    "e2": ((("M2", "f2b"),), ()),
-    "na": ((("M3", "f2b"),), (("N2", "f2b"),)),
+    "go": (((S0, W_KV0), (S0, W_KV1), (S0, W_Q)), ((S0, W_KV0), (S0, W_KV1), (S0, W_Q))),
+    "tb": (((M1, W_KV0), (Y1, W_KV0), (Y1, W_KV1), (M1, W_KV1), (S0, W_P), (M2, W_KV0), (Y1, W_Q), (M2, W_KV1), (S0, W_F1A)), ((N1, W_KV0), (E1, W_KV0), (E1, W_KV1), (N1, W_KV1), (E1, W_Q), (S0, W_P), (N2, W_KV0), (N2, W_KV1), (Y1, W_KV0), (Y1, W_Q), (N1, W_Q), (N2, W_Q), (E1, W_P), (S0, W_F1A))),
+    "tk": (((M3, W_KV0), (M1, W_Q)), ((Y1, W_KV1),)),
+    "w0": (((M3, W_KV1), (Y1, W_F1A), (M2, W_Q), (Y1, W_P), (M3, W_Q), (S0, W_F1B), (M1, W_F1A)), ()),
+    "w1": (((M2, W_P), (M1, W_P)), ((N1, W_P), (N2, W_P), (Y1, W_P), (E1, W_F1A))),
+    "sr": (((M3, W_P), (S0, W_F2A)), ((S0, W_F1B),)),
+    "a0": ((), ((N2, W_F1A),)),
+    "r0": (((Y1, W_F1B),), ()),
+    "a4": (((M3, W_F1A),), ()),
+    "a5": ((), ((N1, W_F1A),)),
+    "a8": (((Y1, W_F2A), (M2, W_F1A), (S0, W_F2B)), ((N1, W_F1B), (S0, W_F2A))),
+    "a10": ((), ((E1, W_F1B),)),
+    "a12": (((M2, W_F1B),), ((Y1, W_F1A),)),
+    "r3": ((), ((N1, W_F2A),)),
+    "rr": (((S0, W_F2C), (M1, W_F1B), (M2, W_F2A), (M1, W_F2A)), ((E1, W_F2A), (N2, W_F1B), (S0, W_F2B), (N2, W_F2A))),
+    "nm": (((Y1, W_F2B), (M3, W_F1B), (Y1, W_F2C), (M3, W_F2A)), ((Y1, W_F1B), (S0, W_F2C))),
+    "e0": (((M1, W_F2C),), ((N1, W_F2B),)),
+    "e1": (((M2, W_F2B),), ((E1, W_F2C), (N1, W_F2C), (E1, W_F2B), (N2, W_F2C))),
+    "e2": (((M2, W_F2C),), ((N2, W_F2B), (Y1, W_F2C), (Y1, W_F2B))),
+    "e3": (((M3, W_F2C),), ((Y1, W_F2A),)),
+    "n0": (((M3, W_F2B),), ()),
+    "n1": (((M1, W_F2B),), ()),
 }
 
 
@@ -428,16 +430,17 @@
     )
 
 
-START = ((("E1", "inner"), ("Y1", "pair")), (("M1", "outer"), ("N1", "inner"), ("Y1", "pair")))
+INNER, OUTER, PAIR = "inner", "outer", "pair"
+START = (((E1, INNER), (Y1, PAIR)), ((M1, OUTER), (N1, INNER), (Y1, PAIR)))
 RELAY = {
-    (0, "M1"): (("Y4", 1, "pair", 0),),
-    (0, "Y1"): (("E2", "pair", "inner", None),),
-    (0, "M2"): (("Y2", 2, "pair", None),),
-    (0, "M3"): (("Y3", 3, "pair", None),),
-    (1, "N1"): (("M2", 1, "outer", None), ("Y2", 1, "pair", None)),
-    (1, "E1"): (("N2", "outer", "inner", None),),
-    (1, "Y1"): (("M4", "pair", "outer", 1),),
-    (1, "N2"): (("M3", 2, "outer", None), ("Y3", 2, "pair", None)),
+    (0, M1): ((Y4, 1, PAIR, 0),),
+    (0, Y1): ((E2, PAIR, INNER, None),),
+    (0, M2): ((Y2, 2, PAIR, None),),
+    (0, M3): ((Y3, 3, PAIR, None),),
+    (1, N1): ((M2, 1, OUTER, None), (Y2, 1, PAIR, None)),
+    (1, E1): ((N2, OUTER, INNER, None),),
+    (1, Y1): ((M4, PAIR, OUTER, 1),),
+    (1, N2): ((M3, 2, OUTER, None), (Y3, 2, PAIR, None)),
 }
 
 
@@ -454,10 +457,12 @@
         self.inner = (z + step) * 2 + y
         self.outer = lax.rem((z - step) * 2 + y + dp, dp)
         middle = lax.rem(lax.div(z + 1, 2), 2)
-        self.far = [(z + step * (k - middle)) * 2 for k in (2, 3)]
+        self.turns = [
+            z + step * (a + middle * (b - a)) for a, b in ((0, 0), (2, -1), (3, 1), (1, 2))
+        ]
         self.ahead = [lax.rem((z + step * k) * 2 + y + dp, dp) for k in range(4)]
         self.homes, self.send, self.recv, self.local = homes, send, recv, local
-        self.peers = {"inner": self.inner, "outer": self.outer, "pair": self.pair}
+        self.peers = {INNER: self.inner, OUTER: self.outer, PAIR: self.pair}
 
     def block(self, name, owner, part=None):
         _, target, stride, low, count = self.homes[name]
@@ -495,7 +500,7 @@
         )
 
     def act(self, role, what, name):
-        if what == "s0":
+        if what == S0:
             here = self.block(name, self.me)
             for kind, peer in START[role]:
                 own = here if self.own(name) is None else self.own(name)
@@ -505,7 +510,7 @@
             return
         self.arrived(name, what)
         for kind, owner, peer, part in RELAY[role, what]:
-            who = {"pair": self.pair, "outer": self.outer}.get(owner)
+            who = {PAIR: self.pair, OUTER: self.outer}.get(owner)
             self.move(name, kind, self.ahead[owner] if who is None else who, peer, part)
 
     def serve(self, point, when=None):
@@ -531,6 +536,20 @@
         def _():
             self.arrived(name, "E2")
 
+    def pair_ready(self, name, turn):
+        if turn == 0:
+            if self.own(name) is not None:
+                self.stay(name).wait()
+            return
+
+        @pl.when(self.end)
+        def _():
+            self.arrived(name, *(("Y2",), ("Y3",), ("Y4", "M4"))[turn - 1])
+
+        @pl.when(self.mid)
+        def _():
+            self.arrived(name, *(("E2",), ("Y2",), ("Y3",))[turn - 1])
+
     def full(self, name):
         self.near(name)
         self.arrived(name, "Y2", "Y3")
@@ -561,16 +580,15 @@
 def layer_kernel(dp, mp, kept_own, *refs):
     (tokens, sizes, gain_one, qkv, proj, gain_two, fc1, bias, fc2, source, target, order) = refs[:12]
     out = refs[12]
-    (tok, raw_qkv, raw_proj, whole, wkv, wpq, w1, w2, shares, picks, own_share, source_share,
+    (tok, raw_qkv, raw_proj, whole, wkv, packed_q, packed_p, wq, wp, w1, w2, shares, picks, own_share, source_share,
      kbuf, vbuf, qall, qbuf, source_att, attb, joined, parts, landing, merged, again, hidden,
-     near_parts, near_landing, far_parts, far_landing, far_own,
+     merged_out, ready_out, landing_out, own_out, done_out,
      send, recv, local, msend, mrecv) = refs[13:]
     rows, width = tok.shape
     length = sizes.shape[1]
     local_width = joined.shape[1]
     local_heads, _, lanes = kbuf.shape
     head_size = local_width // local_heads
-    half = width // 2
     at = lax.axis_index("mp")
     block_of = [toggled(at, k) for k in range(mp)]
     pair, across = block_of[1], block_of[2]
@@ -580,12 +598,19 @@
     homes = {
         "kv0": (None, lambda r: wkv.at[r, :], shard, 0, shard // 2),
         "kv1": (None, lambda r: wkv.at[r, :], shard, shard // 2, shard // 2),
-        "pq0": (None, lambda r: wpq.at[r, :], shard, 0, shard // 2),
-        "pq1": (None, lambda r: wpq.at[r, :], shard, shard // 2, shard // 2),
+        "q": (None, lambda r: packed_q.at[r, :], shard // 2, 0, shard // 2),
+        "p": (None, lambda r: packed_p.at[r, :], shard // 2, 0, shard // 2),
         "f1a": (fc1.at[:, pl.ds(0, cut)], lambda r: w1.at[r, pl.ds(0, cut)], shard, 0, shard),
         "f1b": (fc1.at[:, pl.ds(cut, cut)], lambda r: w1.at[r, pl.ds(cut, cut)], shard, 0, shard),
         "f2a": (fc2.at[:, pl.ds(0, cut)], lambda r: w2.at[r, pl.ds(0, cut)], shard, 0, shard),
-        "f2b": (fc2.at[:, pl.ds(cut, cut)], lambda r: w2.at[r, pl.ds(cut, cut)], shard, 0, shard),
+        "f2b": (
+            fc2.at[pl.ds(0, shard // 2), pl.ds(cut, cut)],
+            lambda r: w2.at[r, pl.ds(cut, cut)], shard, 0, shard // 2,
+        ),
+        "f2c": (
+            fc2.at[pl.ds(shard // 2, shard // 2), pl.ds(cut, cut)],
+            lambda r: w2.at[r, pl.ds(cut, cut)], shard, shard // 2, shard // 2,
+        ),
     }
     st = Streams(dp, homes, send, recv, local)
 
@@ -617,8 +642,21 @@
     mine = pl.ds(pl.multiple_of(st.me * shard, shard), shard)
     wkv[mine, 0:local_width] = raw_qkv[1]
     wkv[mine, local_width : 2 * local_width] = raw_qkv[2]
-    wpq[mine, 0:local_width] = raw_proj[...]
-    wpq[mine, local_width : 2 * local_width] = raw_qkv[0]
+    few = shard // 2
+    mine = pl.ds(pl.multiple_of(st.me * few, few), few)
+    for packed, raw in ((packed_q, raw_qkv.at[0]), (packed_p, raw_proj)):
+        packed[mine, 0:local_width] = raw[0:few]
+        packed[mine, local_width : 2 * local_width] = raw[few:shard]
+
+    def unpack(packed, flat):
+        def one(owner, carry):
+            there = pl.ds(pl.multiple_of(owner * few, few), few)
+            for side in range(2):
+                here = pl.ds(pl.multiple_of(owner * shard + side * few, few), few)
+                flat[here, :] = packed[there, side * local_width : (side + 1) * local_width]
+            return carry
+
+        lax.fori_loop(0, dp, one, 0)
 
     @pl.when(st.end)
     def _():
@@ -719,13 +757,10 @@
             vbuf[h, span, 0:head_size] = product[:, low : low + head_size]
         return carry
 
-    skip = local_width % 128
     factor = LOG2E / math.sqrt(head_size)
 
     def project_q(b, carry):
-        product = jnp.dot(
-            whole[b], wpq[:, local_width - skip :], preferred_element_type=jnp.float32
-        )
+        product = jnp.dot(whole[b], wq[...], preferred_element_type=jnp.float32)
         span = pl.ds(pl.multiple_of(b * rows, rows), rows)
         qall[span, :] = (product * factor).astype(jnp.bfloat16)
         return carry
@@ -735,14 +770,14 @@
     st.full("kv1")
     lax.fori_loop(0, mp, project_kv, 0)
     st.serve("w1")
-    st.full("pq0")
-    st.full("pq1")
+    st.full("q")
+    unpack(packed_q, wq)
     lax.fori_loop(0, mp, project_q, 0)
 
     def heads_of(product):
         chosen = product.astype(jnp.bfloat16)
         for h in range(local_heads):
-            low = skip + h * head_size
+            low = h * head_size
             yield h, chosen[:, low : low + head_size]
 
     def mix(query, h):
@@ -781,8 +816,11 @@
         for h in range(local_heads):
             joined[:, h * head_size : (h + 1) * head_size] = attb[h, :, 0:head_size]
         st.serve(f"r{turn}")
+        if turn == 0:
+            st.full("p")
+            unpack(packed_p, wp)
         kept = shares[block, :, pl.ds(pl.multiple_of(at * rows, rows), rows)]
-        return nt_dot(joined[...], wpq[:, 0:local_width]) + jnp.dot(
+        return nt_dot(joined[...], wp[...]) + jnp.dot(
             kept, tok[...], preferred_element_type=jnp.float32
         )
 
@@ -813,6 +851,8 @@
     lax.fori_loop(0, rows // slab, norm_again, 0)
     norm_pair = give(again.at[at], again.at[at], pair)
     norm_across = give(again.at[at], again.at[at], across)
+    for column in range(4):
+        merged_out[column] = merged[:, column * 2 * shard : (column + 1) * 2 * shard]
     st.serve("nm")
     st.full("f1a")
     st.full("f1b")
@@ -835,54 +875,44 @@
     expand(block_of[3])
     st.serve("e3")
 
-    near = lax.div(lax.div(st.me, 2), 2)
-
-    def shrink(start, size, ready, landed):
-        columns = pl.ds(pl.multiple_of(start, shard), size)
+    quarter = 2 * shard
+
+    def fold(values):
+        return jnp.concatenate([values[: rows // 2], values[rows // 2 :]], axis=1)
+
+    def unfold(values):
+        return jnp.concatenate([values[:, :quarter], values[:, quarter:]], axis=0)
+
+    flights = []
+    for turn in range(4):
+        for name in DOWN:
+            st.pair_ready(name, turn)
+        columns = pl.ds(pl.multiple_of(st.turns[turn] * quarter, quarter), quarter)
+        ready, landed = ready_out.at[turn], landing_out.at[turn]
 
         def piece(block):
             return nt_dot(hidden[block], w2[columns, :])
 
-        ready[2] = piece(block_of[3]).astype(jnp.bfloat16)
+        ready[2] = fold(piece(block_of[3])).astype(jnp.bfloat16)
         one = give(ready.at[2], landed.at[2], pair)
-        total = piece(across)
+        ready[0] = fold(piece(pair)).astype(jnp.bfloat16)
+        three = give(ready.at[0], landed.at[0], pair)
+        total = fold(piece(across))
         one.wait_recv()
         ready[1] = (total + landed[2].astype(jnp.float32)).astype(jnp.bfloat16)
         two = give(ready.at[1], landed.at[1], across)
-        ready[0] = piece(pair).astype(jnp.bfloat16)
-        three = give(ready.at[0], landed.at[0], pair)
-        return piece(at), two, three
-
-    def landed_sum(landed):
-        return landed[0].astype(jnp.float32) + landed[1].astype(jnp.float32)
-
-    st.near("f2a")
-    st.near("f2b")
-    span = pl.ds(pl.multiple_of(near * half, half), half)
-    total, *close = shrink(near * half, half, near_parts, near_landing)
-    merged[:, span] = merged[:, span] + total
-    st.serve("na")
-    flights = []
-    for number, kind in ((0, "Y2"), (1, "Y3")):
-        st.arrived("f2a", kind)
-        st.arrived("f2b", kind)
-        total, *flight = shrink(
-            lax.div(st.far[number], 2) * 2 * shard, 2 * shard, far_parts.at[number],
-            far_landing.at[number],
-        )
-        far_own[number] = total
-        flights += flight
-        st.serve(("nc", "nd")[number])
-    for flight in close:
-        flight.wait_recv()
-    out[:, span] = (merged[:, span] + landed_sum(near_landing)).astype(out.dtype)
-    for flight in flights:
-        flight.wait_recv()
-    span = pl.ds(pl.multiple_of((1 - near) * half, half), half)
-    sides = [
-        far_own[side] + landed_sum(far_landing.at[side]) for side in (near, 1 - near)
-    ]
-    out[:, span] = (merged[:, span] + jnp.concatenate(sides, axis=1)).astype(out.dtype)
+        own_out[turn] = merged_out[st.turns[turn]] + piece(at)
+        st.serve(f"n{turn}")
+        flights.append((three, two))
+    for turn, flight in enumerate(flights):
+        for copy in flight:
+            copy.wait_recv()
+        landed = landing_out[turn, 0].astype(jnp.float32) + landing_out[turn, 1].astype(
+            jnp.float32
+        )
+        done_out[st.turns[turn]] = (own_out[turn] + unfold(landed)).astype(jnp.bfloat16)
+    for column in range(4):
+        out[:, column * quarter : (column + 1) * quarter] = done_out[column]
     for name in ARRAYS:
         st.sent(name)
     for copy in made:
@@ -903,16 +933,17 @@
     bf16, f32 = jnp.bfloat16, jnp.float32
     vmem = pl.BlockSpec(memory_space=pltpu.VMEM)
     hbm = pl.BlockSpec(memory_space=pl.ANY)
-    half = width // 2
     shard, count = fc1_weight.shape[0], pair_source.shape[1]
-    whole_q = local_width + local_width % 128
     scratch = [
         pltpu.VMEM((rows, width), bf16),
         pltpu.VMEM((3, shard, local_width), bf16),
         pltpu.VMEM((shard, local_width), bf16),
         pltpu.VMEM((mp, rows, width), bf16),
         pltpu.VMEM((width, 2 * local_width), bf16),
-        pltpu.VMEM((width, 2 * local_width), bf16),
+        pltpu.VMEM((width // 2, 2 * local_width), bf16),
+        pltpu.VMEM((width // 2, 2 * local_width), bf16),
+        pltpu.VMEM((width, local_width), bf16),
+        pltpu.VMEM((width, local_width), bf16),
         pltpu.VMEM((width, hidden), bf16),
         pltpu.VMEM((width, hidden), bf16),
         pltpu.VMEM((mp, rows, length), bf16),
@@ -921,7 +952,7 @@
         pltpu.VMEM((mp, rows, count), bf16),
         pltpu.VMEM((local_heads, length, lanes), bf16),
         pltpu.VMEM((local_heads, length, lanes), bf16),
-        pltpu.VMEM((length, whole_q), bf16),
+        pltpu.VMEM((length, local_width), bf16),
         pltpu.VMEM((local_heads, rows, lanes), bf16),
         pltpu.VMEM((local_heads, count, lanes), bf16),
         pltpu.VMEM((local_heads, rows, lanes), bf16),
@@ -931,16 +962,16 @@
         pltpu.VMEM((rows, width), f32),
         pltpu.VMEM((mp, rows, width), bf16),
         pltpu.VMEM((mp, rows, hidden), bf16),
-        pltpu.VMEM((mp - 1, rows, half), bf16),
-        pltpu.VMEM((mp - 1, rows, half), bf16),
-        pltpu.VMEM((2, mp - 1, rows, 2 * shard), bf16),
-        pltpu.VMEM((2, mp - 1, rows, 2 * shard), bf16),
-        pltpu.VMEM((2, rows, 2 * shard), f32),
+        pltpu.VMEM((4, rows, 2 * shard), f32),
+        pltpu.VMEM((4, mp - 1, rows // 2, 4 * shard), bf16),
+        pltpu.VMEM((4, mp - 1, rows // 2, 4 * shard), bf16),
+        pltpu.VMEM((4, rows, 2 * shard), f32),
+        pltpu.VMEM((4, rows, 2 * shard), bf16),
         pltpu.SemaphoreType.DMA((len(ARRAYS) * len(KINDS),)),
         pltpu.SemaphoreType.DMA((len(ARRAYS) * len(KINDS),)),
         pltpu.SemaphoreType.DMA((len(ARRAYS) + 3,)),
-        pltpu.SemaphoreType.DMA((18,)),
-        pltpu.SemaphoreType.DMA((18,)),
+        pltpu.SemaphoreType.DMA((24,)),
+        pltpu.SemaphoreType.DMA((24,)),
     ]
     out = pl.pallas_call(
         functools.partial(layer_kernel, dp, mp, kept_own),

time: 121 us -> 116 us (0.959)
  Pallas kernels: 119 us -> 114 us
    pallas_call x1, Pallas kernels: 119 us -> 114 us  [whole_layer(): pl.pallas_call(functools.partial(layer_kernel, dp, mp, kept_own), out_sha...]
where the time goes in v3:
time: 116 us
  Pallas kernels  114 us (98%)
  local copies, waits for them, and re-layouts  1.97 us (2%)
    pallas_call x1, Pallas kernels, whole_layer(): pl.pallas_call(functools.partial(layer_kernel, dp, mp, kept_own), out_sha...  114 us

profile of v3, /device:TPU:0, one launch (start us, length us, event | category | flops | bytes accessed | tf_op | source)
XLA Modules:
  0.0 116.0 jit_solution(5527536020373003245)
XLA Ops:
  0.0 114.0 %layer.1 = bf16[256,1280]{1,0:T(8,128)(2,1)} custom-call(bf16[256,1280]{1,0:T(8,128)(2,1)} %bitcast.5, f32[1,1024]{1,0:T(1,128)} %refs_1_.1, f32[1280]{0:T(1024)} %refs_2_.1, bf16[3,160,320]{2,1,0:T(8,128)(2,1)} %refs_3_.1, bf16[160,320]{1,0:T(8,128)(2,1)} %bitcast.7, f32[1280]{0:T(1024)} %refs_5_.1, bf16[160,1280]{1,0:T(8,128)(2,1)} %refs_6_.1, ...), custom_call_target="tpu_custom_call" | custom-call | flops 10000000000 | bytes 100000000 | tf_op jit(solution)/shard_map/layer/pallas_call | solution.py:976
  114.1 2.0 %slice_bitcast_fusion = bf16[1,252,1280]{2,1,0:T(8,128)(2,1)} fusion(bf16[256,1280]{1,0:T(8,128)(2,1)} %layer.1), kind=kLoop, calls=%fused_computation | loop fusion | bytes 1290240 | tf_op jit(solution)/shard_map/broadcast_in_dim | solution.py:1001
